TPU v7x, 32 devices: a whole 2x2x4 slice. The times are simulated.
32 devices in a mesh: dop: 2 (over core), tm: 16 (over z, y, x).
Axes of the slice: x: 2, y: 2, z: 4, core: 2. Of those that a mesh axis runs over, the one named last changes fastest.
Arguments:
- surveillance: bfloat16 [2, 16, 8192], P(None, 'tm', 'dop'), may hold values from -6 to 6
- reference_signal: bfloat16 [2, 16, 8192], P(None, 'tm', 'dop'), may hold values from -6 to 6
Outputs:
- ambiguity: float32 [2048, 2, 512], P('tm', None, 'dop')
All inputs are finite; a program needn't handle non-finite values.
Results may differ from a plain program's by a relative error of at most 0.0029.
Values may be sent and summed in bfloat16 or wider, within the bound.
A program may use at most 128 MiB of HBM per device.

v0:
```python
import math

import jax
import jax.numpy as jnp
import numpy as np
from jax import lax
from jax.experimental import pallas as pl
from jax.experimental.pallas import tpu as pltpu
from jax.sharding import PartitionSpec as P

F = 512
LAGS = 2048
BLOCK = 8192
STRIDED = 2048
GROUP = 4


def tables(window):
    depth = STRIDED
    phases = window // depth
    half = F // 2
    q = np.arange(half, dtype=np.float64) + 0.5
    b = np.arange(depth, dtype=np.float64)
    a = np.arange(phases, dtype=np.float64)
    inner = 2.0 * np.pi / depth * np.mod(b[:, None] * q[None, :], depth)
    waves = np.concatenate([np.cos(inner), np.sin(inner)], 1).astype(jnp.bfloat16)
    outer = 2.0 * np.pi / window * a[:, None] * q[None, :]
    scale = 1.0 / math.sqrt(window)
    turns = (np.stack([np.cos(outer), np.sin(outer)]) * scale).astype(np.float32)
    half_b = np.pi / depth * b[None, :]
    half_a = np.pi / window * a[:, None]
    return waves, turns, half_a, half_b


def kernel(lags, s_ref, r_ref, waves_ref, turns_ref, out_ref, shifted, y0, y1, u0, u1):
    phases, depth = s_ref.shape[1:]
    half = turns_ref.shape[2]
    rows = shifted.shape[2]
    per_eight = 8 // GROUP
    groups = lags // GROUP

    @pl.loop(0, 2 * (depth // 512))
    def _(turn):
        part = turn % 2
        lanes = pl.ds(pl.multiple_of(turn // 2 * 512, 512), 512)
        for early in range(8):
            for row in range(0, rows, 8):
                shifted[early, part, row : row + 8, lanes] = r_ref[
                    part, row + 8 - early : row + 16 - early, lanes
                ]

    def build(group, y):
        eight = group // per_eight
        first = (group % per_eight) * GROUP
        start = lags - 8 - 8 * eight
        for row in range(0, phases, 16):
            here = pl.ds(pl.multiple_of(start + row, 8), 16)
            for lane in range(0, depth, 256):
                lanes = slice(lane, lane + 256)
                sr = s_ref[0, row : row + 16, lanes]
                si = s_ref[1, row : row + 16, lanes]
                for i in range(GROUP):
                    rr = shifted[first + i, 0, here, lanes]
                    ri = shifted[first + i, 1, here, lanes]
                    at = 2 * i * phases + row
                    y[at : at + 16, lanes] = (sr * rr + si * ri).astype(jnp.bfloat16)
                    at += phases
                    y[at : at + 16, lanes] = (si * rr - sr * ri).astype(jnp.bfloat16)

    def transform(y, u):
        u[...] = jnp.dot(y[...], waves_ref[...], preferred_element_type=jnp.float32)

    def gather_phases(group, u):
        for i in range(GROUP):
            for lane in range(0, half, 128):
                cos_lanes = slice(lane, lane + 128)
                sin_lanes = slice(half + lane, half + lane + 128)
                sums = [jnp.zeros((8, 128), jnp.float32) for _ in range(4)]
                for row in range(0, phases, 8):
                    c = turns_ref[0, row : row + 8, cos_lanes]
                    s = turns_ref[1, row : row + 8, cos_lanes]
                    at = 2 * i * phases + row
                    p1 = u[at : at + 8, cos_lanes]
                    p4 = u[at : at + 8, sin_lanes]
                    p3 = u[at + phases : at + phases + 8, cos_lanes]
                    p2 = u[at + phases : at + phases + 8, sin_lanes]
                    sums[0] += p1 * c - p4 * s
                    sums[1] += p2 * c + p3 * s
                    sums[2] += p3 * c - p2 * s
                    sums[3] += p4 * c + p1 * s
                al, be, ga, de = [jnp.sum(v, axis=0, keepdims=True) for v in sums]
                out_ref[group * GROUP + i, :, cos_lanes] = jnp.concatenate(
                    [al + be, ga - de, al - be, ga + de], 0
                )

    build(0, y0)

    @pl.loop(0, groups // 2)
    def _(pair):
        even = pair * 2
        transform(y0, u0)
        build(even + 1, y1)
        gather_phases(jnp.maximum(even - 1, 0), u1)
        transform(y1, u1)
        build(jnp.minimum(even + 2, groups - 1), y0)
        gather_phases(even, u0)

    gather_phases(groups - 1, u1)


def ambiguity_lags(signal, reference, first_lag, lags, interpret=False):
    window = signal.shape[1]
    depth = STRIDED
    phases = window // depth
    half = F // 2
    waves, turns, half_a, half_b = tables(window)

    strided = signal.reshape(2, depth, phases).transpose(0, 2, 1).astype(jnp.float32)
    ca, sa = [jnp.asarray(f(half_a), jnp.float32) for f in (np.cos, np.sin)]
    cb, sb = [jnp.asarray(f(half_b), jnp.float32) for f in (np.cos, np.sin)]
    c = ca * cb - sa * sb
    s = sa * cb + ca * sb
    turned = jnp.stack(
        [strided[0] * c - strided[1] * s, strided[1] * c + strided[0] * s]
    )

    padded = jnp.pad(reference, ((0, 0), (LAGS, phases)))
    delayed = lax.dynamic_slice_in_dim(
        padded, LAGS - lags - first_lag, window + phases, 1
    )
    near = delayed[:, :window].reshape(2, depth, phases)
    far = delayed[:, phases:].reshape(2, depth, phases)[:, :, :lags]
    columns = jnp.concatenate([near, far], 2).transpose(0, 2, 1).astype(jnp.float32)

    tall = GROUP * 2 * phases
    return pl.pallas_call(
        lambda *refs: kernel(lags, *refs),
        out_shape=jax.ShapeDtypeStruct((lags, 4, half), jnp.float32),
        in_specs=[pl.BlockSpec(memory_space=pltpu.VMEM)] * 4,
        out_specs=pl.BlockSpec(memory_space=pltpu.VMEM),
        scratch_shapes=[
            pltpu.VMEM((8, 2, phases + lags - 8, depth), jnp.float32),
            pltpu.VMEM((tall, depth), jnp.bfloat16),
            pltpu.VMEM((tall, depth), jnp.bfloat16),
            pltpu.VMEM((tall, F), jnp.float32),
            pltpu.VMEM((tall, F), jnp.float32),
        ],
        compiler_params=pltpu.CompilerParams(vmem_limit_bytes=56 * 1024 * 1024),
        interpret=interpret,
    )(turned, columns, jnp.asarray(waves), jnp.asarray(turns))


def flipped(index, bit):
    weight = 1 << bit
    return index + weight * (1 - 2 * ((index // weight) % 2))


def spread_kernel(orders, cuts, *refs):
    count = len(orders)
    own, every = refs[:count], refs[count : 2 * count]
    send_sems, recv_sems = refs[2 * count :]
    me = lax.axis_index("tm") * cuts + lax.axis_index("dop")

    def place(index):
        return {"tm": index // cuts, "dop": index % cuts}

    barrier = pltpu.get_barrier_semaphore()
    for bit in orders[0]:
        pl.semaphore_signal(
            barrier,
            inc=1,
            device_id=place(flipped(me, bit)),
            device_id_type=pl.DeviceIdType.MESH,
        )
    pl.semaphore_wait(barrier, len(orders[0]))

    def copy(which, source, block, slot, target):
        return pltpu.make_async_remote_copy(
            src_ref=source,
            dst_ref=every[which].at[block],
            send_sem=send_sems.at[which, slot],
            recv_sem=recv_sems.at[which, block],
            device_id=place(target),
            device_id_type=pl.DeviceIdType.MESH,
        )

    sent = []
    held = [[me] for _ in orders]
    landed = [1] * count
    for step in range(len(orders[0])):
        partners = [flipped(me, order[step]) for order in orders]
        for at in range(1 << step):
            for which in range(count):
                block = held[which][at]
                mine = every[which].at[block]
                if at == 0:
                    mine = own[which]
                elif at >= landed[which]:
                    copy(which, mine, block, 0, partners[which]).wait_recv()
                    landed[which] = at + 1
                one = copy(which, mine, block, (1 << step) - 1 + at, partners[which])
                one.start()
                sent.append(one)
        for which, order in enumerate(orders):
            held[which] = held[which] + [flipped(h, order[step]) for h in held[which]]
        if step == 0:
            for which in range(count):
                every[which][pl.ds(me, 1)] = own[which][...][None]
    for which in range(count):
        for at in range(landed[which], len(held[which])):
            block = held[which][at]
            copy(which, own[which], block, 0, flipped(me, 0)).wait_recv()
    for one in sent:
        one.wait_send()


def everywhere(values):
    times, cuts = lax.axis_size("tm"), lax.axis_size("dop")
    devices = times * cuts
    bits = devices.bit_length() - 1
    shape = values[0].shape
    order = list(range(bits))[::-1]
    other = order[:-3] + [order[-2], order[-3], order[-1]]
    rows = shape[0] * shape[1] * shape[2] // 128
    block = jax.ShapeDtypeStruct((devices, rows, 128), values[0].dtype)
    gathered = pl.pallas_call(
        lambda *refs: spread_kernel([order, other], cuts, *refs),
        out_shape=[block] * 2,
        in_specs=[pl.BlockSpec(memory_space=pltpu.VMEM)] * 2,
        out_specs=[pl.BlockSpec(memory_space=pltpu.VMEM)] * 2,
        scratch_shapes=[
            pltpu.SemaphoreType.DMA((2, devices)),
            pltpu.SemaphoreType.DMA((2, devices)),
        ],
        compiler_params=pltpu.CompilerParams(collective_id=0, has_side_effects=True),
    )(*[value.reshape(rows, 128) for value in values])
    return [
        every.reshape((times, cuts) + shape)
        .transpose(2, 0, 3, 1, 4)
        .reshape(2, devices * shape[1] * shape[2])
        for every in gathered
    ]


def swap_kernel(cuts, parts, out, send_sems, recv_sems):
    me = lax.axis_index("dop")
    partners = [me]
    for bit in range(cuts.bit_length() - 1):
        partners = partners + [flipped(p, bit) for p in partners]
    partners = partners[1:]

    barrier = pltpu.get_barrier_semaphore()
    for partner in partners:
        pl.semaphore_signal(
            barrier,
            inc=1,
            device_id={"dop": partner},
            device_id_type=pl.DeviceIdType.MESH,
        )
    pl.semaphore_wait(barrier, len(partners))

    def copy(source, target, owner):
        return pltpu.make_async_remote_copy(
            src_ref=parts.at[source],
            dst_ref=out.at[owner],
            send_sem=send_sems.at[target],
            recv_sem=recv_sems.at[owner],
            device_id={"dop": target},
            device_id_type=pl.DeviceIdType.MESH,
        )

    for partner in partners:
        copy(partner, partner, me).start()
    out[pl.ds(me, 1)] = parts[pl.ds(me, 1)]
    for partner in partners:
        copy(partner, partner, partner).wait_recv()
    for partner in partners:
        copy(partner, partner, me).wait_send()


def swapped(whole):
    cuts = lax.axis_size("dop")
    lags, two, bins = whole.shape
    parts = whole.reshape(lags, two, cuts, bins // cuts).transpose(2, 0, 1, 3)
    flat = parts.reshape(cuts, lags * two, bins // cuts)
    out = pl.pallas_call(
        lambda *refs: swap_kernel(cuts, *refs),
        out_shape=jax.ShapeDtypeStruct(flat.shape, flat.dtype),
        in_specs=[pl.BlockSpec(memory_space=pltpu.VMEM)],
        out_specs=pl.BlockSpec(memory_space=pltpu.VMEM),
        scratch_shapes=[
            pltpu.SemaphoreType.DMA((cuts,)),
            pltpu.SemaphoreType.DMA((cuts,)),
        ],
        compiler_params=pltpu.CompilerParams(collective_id=1, has_side_effects=True),
    )(flat)
    return out.reshape(cuts * lags, two, bins // cuts)


def on_device(surveillance, reference_signal):
    cuts = lax.axis_size("dop")
    lags = LAGS // (lax.axis_size("tm") * cuts)
    first_lag = (lax.axis_index("tm") * cuts + lax.axis_index("dop")) * lags
    signal, reference = everywhere([surveillance, reference_signal])
    found = ambiguity_lags(signal, reference, first_lag, lags)
    whole = jnp.concatenate([found[:, 2:, ::-1], found[:, :2, :]], 2)
    return swapped(whole)


def solution(mesh):
    return jax.shard_map(
        on_device,
        mesh=mesh,
        in_specs=(P(None, "tm", "dop"), P(None, "tm", "dop")),
        out_specs=P("tm", None, "dop"),
        check_vma=False,
    )
```

profile of v0, /device:TPU:1, one launch (start us, length us, event | category | flops | bytes accessed | tf_op | source)
XLA Modules:
  0.0 68.5 jit_solution(13457395994113677589)
XLA Ops:
  0.0 1.3 %reshape.310.refs_0_ = bf16[64,128]{1,0:T(8,128)(2,1)} reshape(bf16[2,1,4096]{2,0,1:T(2,128)(2,1)} %param.8) | data formatting | bytes 32768 | tf_op jit(solution)/shard_map/reshape | solution.py:236
  1.3 1.3 %reshape.311.refs_1_ = bf16[64,128]{1,0:T(8,128)(2,1)} reshape(bf16[2,1,4096]{2,0,1:T(2,128)(2,1)} %param.9) | data formatting | bytes 32768 | tf_op jit(solution)/shard_map/reshape | solution.py:236
  2.7 19.9 %shard_map.82 = (bf16[32,64,128]{2,1,0:T(8,128)(2,1)}, bf16[32,64,128]{2,1,0:T(8,128)(2,1)}) custom-call(bf16[64,128]{1,0:T(8,128)(2,1)} %reshape.310.refs_0_, bf16[64,128]{1,0:T(8,128)(2,1)} %reshape.311.refs_1_), custom_call_target="tpu_custom_call" | custom-call | tf_op jit(solution)/shard_map/pallas_call | solution.py:226
  22.6 1.6 %reshape.320 = f32[16,2,2,1,4096]{4,2,1,0,3:T(2,128)S(1)} reshape(bf16[32,64,128]{2,1,0:T(8,128)(2,1)} %get-tuple-element.7) | data formatting | bytes 1572864 | tf_op jit(solution)/shard_map/convert_element_type | solution.py:118
  24.2 0.9 %copy.18 = f32[16,2,2,1,4096]{4,1,0,2,3:T(2,128)S(1)} copy(f32[16,2,2,1,4096]{4,2,1,0,3:T(2,128)S(1)} %reshape.320) | data formatting | bytes 2097152 | tf_op jit(solution)/shard_map/convert_element_type | solution.py:118
  25.1 1.2 %reshape.319 = f32[2,2048,64]{2,1,0:T(8,128)S(1)} reshape(f32[2,16,1,2,4096]{4,3,1,0,2:T(2,128)S(1)} %bitcast.22) | data formatting | bytes 2097152 | tf_op jit(solution)/shard_map/convert_element_type | solution.py:118
  26.3 0.0 copy-start.1
  26.3 0.0 copy-start.2
  26.3 0.0 copy-start.3
  26.3 0.0 copy-start.4
  26.3 0.6 copy.11
  26.9 0.1 copy-done.1
  27.0 0.0 copy-done.2
  27.0 0.0 copy-done.3
  27.0 0.0 copy-done.4
  27.0 0.0 copy-start
  27.0 0.3 multiply_subtract_fusion
  27.3 1.1 %pad_maximum_fusion.refs_0_ = f32[2,64,2048]{2,1,0:T(8,128)} fusion(f32[1,64,2048]{2,1,0:T(8,128)S(1)} %get-tuple-element.10, f32[1,64,2048]{2,1,0:T(8,128)S(1)} %get-tuple-element.9), kind=kLoop, calls=%fused_computation.1 | loop fusion | flops 262144 | bytes 2097152 | tf_op jit(solution)/shard_map/stack | solution.py:123
  28.4 0.0 copy-done
  28.4 0.1 reshape.312
  28.5 1.5 %pad_dynamic-slice_fusion = (bf16[2,131072]{1,0:T(2,128)(2,1)S(1)}, bf16[2,131072]{1,0:T(2,128)(2,1)S(1)}) fusion(s32[]{:T(128)S(6)} %select_n.3, bf16[2,131072]{1,0:T(2,128)(2,1)S(1)} %bitcast.24, s32[]{:T(128)S(6)} %add.28), kind=kLoop, calls=%fused_computation.7 | loop fusion | bytes 1572872 | tf_op jit(solution)/shard_map/slice | solution.py:131
  30.0 0.7 reshape.315
  30.7 0.3 copy.13
  31.0 0.7 reshape.314
  31.7 0.3 copy.12
  32.0 1.6 %convert_bitcast_fusion.refs_1_ = f32[2,128,2048]{2,1,0:T(8,128)} fusion(bf16[2,2048,64]{1,2,0:T(8,128)(2,1)S(1)} %copy.13, bf16[2,2048,64]{1,2,0:T(8,128)(2,1)S(1)} %copy.12), kind=kLoop, calls=%fused_computation | loop fusion | flops 2097152 | bytes 3145728 | tf_op jit(solution)/shard_map/convert_element_type | solution.py:133
  33.6 27.4 %shard_map.83 = f32[64,4,256]{2,1,0:T(4,128)} custom-call(f32[2,64,2048]{2,1,0:T(8,128)} %pad_maximum_fusion.refs_0_, f32[2,128,2048]{2,1,0:T(8,128)} %convert_bitcast_fusion.refs_1_, bf16[2048,512]{1,0:T(8,128)(2,1)} %constant.38.clone.refs_2_, f32[2,64,256]{2,1,0:T(8,128)} %constant.39.clone.refs_3_), custom_call_target="tpu_custom_call" | custom-call | tf_op jit(solution)/shard_map/pallas_call | solution.py:136
  61.0 1.1 %fusion = (f32[64,2,256]{2,1,0:T(2,128)S(1)}, f32[64,2,256]{2,1,0:T(2,128)S(1)}) fusion(f32[64,4,256]{2,1,0:T(4,128)} %shard_map.83), kind=kLoop, calls=%fused_computation.11 | loop fusion | bytes 524288 | tf_op jit(solution)/shard_map/slice | solution.py:306
  62.1 0.4 rev.3
  62.6 0.1 pad_maximum_fusion.1
  62.7 0.9 %reshape.317.refs_0_ = f32[2,128,256]{2,1,0:T(8,128)} reshape(f32[2,64,2,256]{3,2,1,0:T(2,128)S(1)} %bitcast.26) | data formatting | bytes 524288 | tf_op jit(solution)/shard_map/reshape | solution.py:285
  63.6 3.0 %shard_map.84 = f32[2,128,256]{2,1,0:T(8,128)} custom-call(f32[2,128,256]{2,1,0:T(8,128)} %reshape.317.refs_0_), custom_call_target="tpu_custom_call" | custom-call | tf_op jit(solution)/shard_map/pallas_call | solution.py:286
  66.7 1.8 %reshape.318 = f32[128,2,256]{2,1,0:T(2,128)} reshape(f32[2,128,256]{2,1,0:T(8,128)} %shard_map.84) | data formatting | bytes 524288 | tf_op jit(solution)/shard_map/reshape | solution.py:297
  (1 shorter events, 0.0 us)
Async XLA Ops:
  26.3 0.7 %copy-start.1 = (f32[2048]{0:T(1024)S(1)}, f32[2048]{0:T(1024)}, u32[]{:S(2)}) copy-start(f32[2048]{0:T(1024)} %constant.47) | copy-start | bytes 24580
  26.3 0.7 %copy-start.2 = (f32[2048]{0:T(1024)S(1)}, f32[2048]{0:T(1024)}, u32[]{:S(2)}) copy-start(f32[2048]{0:T(1024)} %constant.45) | copy-start | bytes 24580
  26.3 0.7 %copy-start.3 = (f32[64]{0:T(128)S(1)}, f32[64]{0:T(128)}, u32[]{:S(2)}) copy-start(f32[64]{0:T(128)} %constant.46) | copy-start | bytes 772
  26.3 0.7 %copy-start.4 = (f32[64]{0:T(128)S(1)}, f32[64]{0:T(128)}, u32[]{:S(2)}) copy-start(f32[64]{0:T(128)} %constant.44) | copy-start | bytes 772
  27.0 1.4 %copy-start = (bf16[32,64,128]{2,1,0:T(8,128)(2,1)S(1)}, bf16[32,64,128]{2,1,0:T(8,128)(2,1)}, u32[]{:S(2)}) copy-start(bf16[32,64,128]{2,1,0:T(8,128)(2,1)} %get-tuple-element.8) | copy-start | bytes 1572868
where the time goes:
time: 69.2 us; the launch traced here: 68.5 us
  Pallas kernels  50.3 us (73%)
  local copies, waits for them, and re-layouts  14.9 us (22%)
  other arithmetic  3.06 us (4%)
    pallas_call x1, Pallas kernels, ambiguity_lags(): pl.pallas_call(lambda *refs: kernel(lags, *refs), out_shape=jax.ShapeDtyp...  27.4 us
    pallas_call x1, Pallas kernels, everywhere(): pl.pallas_call(lambda *refs: spread_kernel([order, other], cuts, *refs),...  19.9 us
    convert_element_type x4, local copies, waits for them, and re-layouts, ambiguity_lags(): signal.reshape(2, depth, phases).transpose(0, 2, 1).astype(jnp.float32)  4.29 us
    pallas_call x1, Pallas kernels, swapped(): pl.pallas_call(lambda *refs: swap_kernel(cuts, *refs), out_shape=jax.Shap...  3.03 us
    reshape x2, local copies, waits for them, and re-layouts, everywhere(): value.reshape(rows, 128)  2.67 us
    reshape x1, local copies, waits for them, and re-layouts, swapped(): return out.reshape(cuts * lags, two, bins // cuts)  1.8 us
    convert_element_type x1, other arithmetic, ambiguity_lags(): jnp.concatenate([near, far], 2).transpose(0, 2, 1).astype(jnp.float32)  1.58 us
    slice x1, local copies, waits for them, and re-layouts, ambiguity_lags(): near = delayed[:, :window].reshape(2, depth, phases)  1.46 us

commit v1 on v0

v1 whole, which is shorter than its diff:
```python
import functools
import math

import jax
import jax.numpy as jnp
import numpy as np
from jax import lax
from jax.experimental import pallas as pl
from jax.experimental.pallas import tpu as pltpu
from jax.sharding import PartitionSpec as P

F = 512
LAGS = 2048
LANES = 128
SUB = 8
POINTS = 2 * LAGS
N1 = LAGS // LANES
F1 = POINTS // LANES
UNIT = 2 * N1 * 2
MESH = pl.DeviceIdType.MESH


class Plan:
    def __init__(self, times, cuts, window):
        self.times, self.cuts, self.window = times, cuts, window
        self.devices = times * cuts
        self.units = window // (2 * LAGS)
        self.groups = self.units // 4
        self.fine = window // POINTS
        self.shifts = F // self.fine
        self.share = self.devices // self.fine
        self.mine = self.shifts // self.share
        self.per_owner = self.shifts // cuts
        self.owners = self.mine // self.per_owner
        self.lags = LAGS // times


def halves(x):
    high = x.astype(jnp.bfloat16)
    low = (x - high.astype(jnp.float32)).astype(jnp.bfloat16)
    return high, low


def tables(plan):
    a = np.arange(LANES)
    angle = 2.0 * np.pi / LANES * np.mod(a[:, None] * a[None, :], LANES)
    c, s = np.cos(angle), np.sin(angle)
    waves = []
    for sign in (-1.0, 1.0):
        full = np.block([[c, sign * s], [-sign * s, c]])
        high = full.astype(jnp.bfloat16)
        low = (full - high.astype(np.float64)).astype(jnp.bfloat16)
        waves += [high, low]
    turn = 2.0 * np.pi / POINTS * np.arange(F1)[:, None] * a[None, :]
    turns = np.stack([np.cos(turn), -np.sin(turn)], 1)
    sign = np.where(
        (np.arange(F1)[:, None] * np.arange(SUB)[None, :]) % 2 == 1, -1.0, 1.0
    )
    forward = (turns[:, :, None, :] * sign[:, None, :, None]).astype(np.float32)
    scale = 1.0 / (POINTS * math.sqrt(plan.window))
    back = (np.stack([np.cos(turn), np.sin(turn)], 1) * scale).astype(np.float32)
    back = np.broadcast_to(back[:, :, None, :], (F1, 2, SUB, LANES)).copy()
    return np.stack(waves), forward, back


def times_(x, y):
    return x[0] * y[0] - x[1] * y[1], x[0] * y[1] + x[1] * y[0]


def plus(x, y):
    return x[0] + y[0], x[1] + y[1]


def minus(x, y):
    return x[0] - y[0], x[1] - y[1]


def turned(x, numerator, denominator, sign):
    eighth = (8 * numerator) % (8 * denominator) / denominator
    if eighth == 0:
        return x
    if eighth == 4:
        return -x[0], -x[1]
    if eighth in (2, 6):
        if (eighth == 2) == (sign > 0):
            return -x[1], x[0]
        return x[1], -x[0]
    angle = 2.0 * math.pi * numerator / denominator
    c, s = math.cos(angle), sign * math.sin(angle)
    return x[0] * c - x[1] * s, x[1] * c + x[0] * s


def dft4(x, sign):
    a, b = plus(x[0], x[2]), minus(x[0], x[2])
    c, d = plus(x[1], x[3]), turned(minus(x[1], x[3]), 1, 4, sign)
    return [plus(a, c), plus(b, d), minus(a, c), minus(b, d)]


def dft16(x, sign):
    inner = [dft4(x[i::4], sign) for i in range(4)]
    out = [None] * 16
    for k in range(4):
        column = [turned(inner[i][k], i * k, 16, sign) for i in range(4)]
        for j, value in enumerate(dft4(column, sign)):
            out[k + 4 * j] = value
    return out


def phases_of(steps, window):
    angle = lax.bitwise_and(steps, window - 1).astype(jnp.float32) * (
        2.0 * math.pi / window
    )
    return jnp.cos(angle), -jnp.sin(angle)


def prepare(plan, fine, drift, even, odd):
    sub = lax.broadcasted_iota(jnp.int32, (SUB, LANES), 0)
    lane = lax.broadcasted_iota(jnp.int32, (SUB, LANES), 1)

    @pl.loop(0, plan.groups)
    def _(group):
        segment = 2 * ((sub // 2) * plan.groups + group) + sub % 2
        c, s = phases_of(fine * (lane + segment * LAGS), plan.window)
        drift[group, 0] = c
        drift[group, 1] = s

    @pl.loop(0, N1)
    def _(row):
        steps = jnp.full((SUB, LANES), fine * LANES * row, jnp.int32)
        c, s = phases_of(steps, plan.window)
        even[row, 0] = c
        even[row, 1] = s
        c, s = phases_of(steps + row * (plan.window // F1), plan.window)
        odd[row, 0] = c
        odd[row, 1] = s


def spread_rows(stage):
    return [
        tuple(stage[pl.ds(2 * n + part, SUB, stride=2 * N1), :] for part in range(2))
        for n in range(N1)
    ]


def turn_and_split(found, parity, forward, high, low):
    for pair in range(N1 // 2):
        both = []
        for e in (2 * pair, 2 * pair + 1):
            f1 = 2 * e + parity
            both.append(times_(found[e], (forward[f1, 0], forward[f1, 1])))
        rows = slice(parity * 128 + pair * 16, parity * 128 + pair * 16 + 16)
        for part in range(2):
            h, l = halves(jnp.concatenate([both[0][part], both[1][part]], 0))
            lanes = slice(part * LANES, (part + 1) * LANES)
            high[rows, lanes] = h
            low[rows, lanes] = l


def lanes_turned(high, low, waves, at):
    return (
        jnp.dot(high[...], waves[at], preferred_element_type=jnp.float32)
        + jnp.dot(low[...], waves[at], preferred_element_type=jnp.float32)
        + jnp.dot(high[...], waves[at + 1], preferred_element_type=jnp.float32)
    )


def signal_group(plan, group, gs, waves, forward, work, S):
    drift, even, odd, stage, high, low = work
    for z in range(4):
        start = pl.multiple_of((z * plan.groups + group) * UNIT, UNIT)
        stage[z * UNIT : (z + 1) * UNIT, :] = gs[pl.ds(start, UNIT), :].astype(
            jnp.float32
        )
    here = (drift[group, 0], drift[group, 1])
    x = [times_(v, here) for v in spread_rows(stage)]
    for parity, table in enumerate((even, odd)):
        y = [times_(x[n], (table[n, 0], table[n, 1])) for n in range(N1)]
        turn_and_split(dft16(y, -1), parity, forward, high, low)
    wide = lanes_turned(high, low, waves, 0)
    reach = plan.shifts // 2
    for f1 in range(F1):
        row = (f1 % 2) * 128 + (f1 // 2) * SUB
        for part in range(2):
            v = wide[row : row + SUB, part * LANES : (part + 1) * LANES]
            S[reach + f1, group, part] = v
            if f1 < reach:
                S[reach + f1 + F1, group, part] = pltpu.roll(v, LANES - 1, 1)
            if f1 >= F1 - reach:
                S[reach + f1 - F1, group, part] = pltpu.roll(v, 1, 1)


def reference_group(plan, group, gr, waves, forward, work, R):
    stage, stage2, high, low = work
    for z in range(4):
        start = pl.multiple_of((z * plan.groups + group) * UNIT, UNIT)
        rows = slice(z * UNIT, (z + 1) * UNIT)
        stage2[rows, :] = gr[pl.ds(start, UNIT), :].astype(jnp.float32)
        stage[rows, :] = gr[pl.ds(start + UNIT // 2, UNIT), :].astype(jnp.float32)
    now, before = spread_rows(stage), spread_rows(stage2)
    y = [plus(a, b) for a, b in zip(now, before)]
    turn_and_split(dft16(y, -1), 0, forward, high, low)
    y = [turned(minus(a, b), n, F1, -1) for n, (a, b) in enumerate(zip(now, before))]
    turn_and_split(dft16(y, -1), 1, forward, high, low)
    wide = lanes_turned(high, low, waves, 0)
    for f1 in range(F1):
        row = (f1 % 2) * 128 + (f1 // 2) * SUB
        for part in range(2):
            R[f1, group, part] = wide[
                row : row + SUB, part * LANES : (part + 1) * LANES
            ]


def fold_rows(values):
    sub = lax.broadcasted_iota(jnp.int32, (SUB, LANES), 0)
    step = 1
    while step < SUB:
        upper = (sub // step) % 2 == 1
        values = [
            jnp.where(upper, b, a) + pltpu.roll(jnp.where(upper, a, b), step, 0)
            for a, b in zip(values[::2], values[1::2])
        ]
        step *= 2
    return values[0]


def cross_spectra(plan, first, S, R, high, low):
    @pl.loop(0, F1)
    def _(f1):
        rr = [R[f1, g, 0] for g in range(plan.groups)]
        ri = [R[f1, g, 1] for g in range(plan.groups)]
        blocks = []
        for owner in range(plan.owners):
            re, im = [], []
            for i in range(SUB):
                if i >= plan.per_owner:
                    re.append(jnp.zeros((SUB, LANES), jnp.float32))
                    im.append(jnp.zeros((SUB, LANES), jnp.float32))
                    continue
                at = f1 + first + owner * plan.per_owner + i
                a = b = None
                for g in range(plan.groups):
                    sr, si = S[at, g, 0], S[at, g, 1]
                    u = sr * rr[g] + si * ri[g]
                    v = si * rr[g] - sr * ri[g]
                    a, b = (u, v) if a is None else (a + u, b + v)
                re.append(a)
                im.append(b)
            blocks.append((fold_rows(re), fold_rows(im)))
        tall = plan.owners * SUB
        rows = pl.ds(pl.multiple_of(f1 * tall, tall), tall)
        for part in range(2):
            h, l = halves(jnp.concatenate([b[part] for b in blocks], 0))
            lanes = slice(part * LANES, (part + 1) * LANES)
            high[rows, lanes] = h
            low[rows, lanes] = l


def to_lags(plan, waves, back, high, low, Z, out):
    Z[...] = lanes_turned(high, low, waves, 2)
    tall = plan.owners * SUB
    for owner in range(plan.owners):
        z = []
        for f1 in range(F1):
            rows = slice(f1 * tall + owner * SUB, f1 * tall + owner * SUB + SUB)
            v = (Z[rows, :LANES], Z[rows, LANES:])
            z.append(times_(v, (back[f1, 0], back[f1, 1])))
        half = F1 // 2
        sums = dft16([plus(z[i], z[i + half]) for i in range(half)], 1)
        gaps = dft16(
            [turned(minus(z[i], z[i + half]), i, F1, 1) for i in range(half)], 1
        )
        for e in range(N1 // 2):
            for parity, found in enumerate((sums, gaps)):
                out[2 * e + parity, owner] = jnp.concatenate(found[e], 0).astype(
                    jnp.bfloat16
                )


def compute_kernel(plan, me, gs, gr, waves, forward, back, out, *scratch):
    drift, even, odd, stage, stage2, high, low, S, R, yhigh, ylow, Z = scratch
    me = me()
    fine = me // plan.share
    first = (me % plan.share) * plan.mine
    prepare(plan, fine, drift, even, odd)

    @pl.loop(0, plan.groups)
    def _(group):
        work = (drift, even, odd, stage, high, low)
        signal_group(plan, group, gs, waves, forward, work, S)
        reference_group(plan, group, gr, waves, forward, (stage, stage2, high, low), R)

    cross_spectra(plan, first, S, R, yhigh, ylow)
    to_lags(plan, waves, back, yhigh, ylow, Z, out)


def lag_maps(plan, me, gs, gr, interpret=False):
    waves, forward, back = tables(plan)
    tall = plan.owners * SUB
    reach = plan.shifts
    f32, bf16 = jnp.float32, jnp.bfloat16
    return pl.pallas_call(
        functools.partial(compute_kernel, plan, me),
        out_shape=jax.ShapeDtypeStruct((N1, plan.owners, 2 * SUB, LANES), bf16),
        in_specs=[pl.BlockSpec(memory_space=pltpu.VMEM)] * 5,
        out_specs=pl.BlockSpec(memory_space=pltpu.VMEM),
        scratch_shapes=[
            pltpu.VMEM((plan.groups, 2, SUB, LANES), f32),
            pltpu.VMEM((N1, 2, SUB, LANES), f32),
            pltpu.VMEM((N1, 2, SUB, LANES), f32),
            pltpu.VMEM((4 * UNIT, LANES), f32),
            pltpu.VMEM((4 * UNIT, LANES), f32),
            pltpu.VMEM((F1 * SUB, 2 * LANES), bf16),
            pltpu.VMEM((F1 * SUB, 2 * LANES), bf16),
            pltpu.VMEM((F1 + reach, plan.groups, 2, SUB, LANES), f32),
            pltpu.VMEM((F1, plan.groups, 2, SUB, LANES), f32),
            pltpu.VMEM((F1 * tall, 2 * LANES), bf16),
            pltpu.VMEM((F1 * tall, 2 * LANES), bf16),
            pltpu.VMEM((F1 * tall, 2 * LANES), f32),
        ],
        compiler_params=pltpu.CompilerParams(vmem_limit_bytes=56 * 1024 * 1024),
        interpret=interpret,
    )(gs, gr, jnp.asarray(waves), jnp.asarray(forward), jnp.asarray(back))


def flipped(index, bit):
    weight = 1 << bit
    return index + weight * (1 - 2 * ((index // weight) % 2))


def spread_kernel(orders, cuts, *refs):
    count = len(orders)
    own, every = refs[:count], refs[count : 2 * count]
    send_sems, recv_sems = refs[2 * count :]
    me = lax.axis_index("tm") * cuts + lax.axis_index("dop")

    def place(index):
        return {"tm": index // cuts, "dop": index % cuts}

    barrier = pltpu.get_barrier_semaphore()
    for bit in orders[0]:
        pl.semaphore_signal(
            barrier,
            inc=1,
            device_id=place(flipped(me, bit)),
            device_id_type=pl.DeviceIdType.MESH,
        )
    pl.semaphore_wait(barrier, len(orders[0]))

    def copy(which, source, block, slot, target):
        return pltpu.make_async_remote_copy(
            src_ref=source,
            dst_ref=every[which].at[block],
            send_sem=send_sems.at[which, slot],
            recv_sem=recv_sems.at[which, block],
            device_id=place(target),
            device_id_type=pl.DeviceIdType.MESH,
        )

    sent = []
    held = [[me] for _ in orders]
    landed = [1] * count
    for step in range(len(orders[0])):
        partners = [flipped(me, order[step]) for order in orders]
        for at in range(1 << step):
            for which in range(count):
                block = held[which][at]
                mine = every[which].at[block]
                if at == 0:
                    mine = own[which]
                elif at >= landed[which]:
                    copy(which, mine, block, 0, partners[which]).wait_recv()
                    landed[which] = at + 1
                one = copy(which, mine, block, (1 << step) - 1 + at, partners[which])
                one.start()
                sent.append(one)
        for which, order in enumerate(orders):
            held[which] = held[which] + [flipped(h, order[step]) for h in held[which]]
        if step == 0:
            for which in range(count):
                every[which][pl.ds(me, 1)] = own[which][...][None]
    for which in range(count):
        for at in range(landed[which], len(held[which])):
            block = held[which][at]
            copy(which, own[which], block, 0, flipped(me, 0)).wait_recv()
    for one in sent:
        one.wait_send()


def everywhere(plan, values):
    bits = plan.devices.bit_length() - 1
    order = list(range(bits))[::-1]
    other = order[:-3] + [order[-2], order[-3], order[-1]]
    rows = values[0].shape[0]
    block = jax.ShapeDtypeStruct((plan.devices, rows, LANES), values[0].dtype)
    gathered = pl.pallas_call(
        functools.partial(spread_kernel, [order, other], plan.cuts),
        out_shape=[block] * 2,
        in_specs=[pl.BlockSpec(memory_space=pltpu.VMEM)] * 2,
        out_specs=[pl.BlockSpec(memory_space=pltpu.VMEM)] * 2,
        scratch_shapes=[
            pltpu.SemaphoreType.DMA((2, plan.devices)),
            pltpu.SemaphoreType.DMA((2, plan.devices)),
        ],
        compiler_params=pltpu.CompilerParams(collective_id=0, has_side_effects=True),
    )(*values)
    return [every.reshape(plan.devices * rows, LANES) for every in gathered]


def deal_kernel(plan, tiles, out, send_sems, recv_sems):
    cuts, times = plan.cuts, plan.times
    t, c = lax.axis_index("tm"), lax.axis_index("dop")
    me = t * cuts + c
    fine = me // plan.share
    base = (me % plan.share) * plan.owners
    mine = c // plan.owners

    barrier = pltpu.get_barrier_semaphore()
    here = fine * 0
    targets = []
    for step in range(times):
        to = (t + step) % times
        for owner in range(plan.owners):
            targets.append((step, owner, to, base + owner))
    for step, owner, to, cut in targets:
        itself = (to == t) & (cut == c)

        @pl.when(jnp.logical_not(itself))
        def _():
            pl.semaphore_signal(
                barrier, inc=1, device_id={"tm": to, "dop": cut}, device_id_type=MESH
            )

    sends_to_me = (base <= c) & (c < base + plan.owners)
    expected = plan.fine - jnp.where(sends_to_me, 1, 0)
    pl.semaphore_wait(barrier, expected)

    def copy(step, owner, to, cut):
        return pltpu.make_async_remote_copy(
            src_ref=tiles.at[to * plan.lags // LANES, owner],
            dst_ref=out.at[fine],
            send_sem=send_sems.at[step, owner],
            recv_sem=recv_sems.at[fine],
            device_id={"tm": to, "dop": cut},
            device_id_type=MESH,
        )

    for step, owner, to, cut in targets:
        itself = (to == t) & (cut == c)

        @pl.when(jnp.logical_not(itself))
        def _():
            copy(step, owner, to, cut).start()

        @pl.when(itself)
        def _():
            out[fine] = tiles[to * plan.lags // LANES, owner]

    for source in range(plan.fine):

        @pl.when((fine != source) | jnp.logical_not(sends_to_me))
        def _():
            pltpu.make_async_remote_copy(
                src_ref=tiles.at[0, 0],
                dst_ref=out.at[source],
                send_sem=send_sems.at[0, 0],
                recv_sem=recv_sems.at[source],
                device_id={"tm": t, "dop": c},
                device_id_type=MESH,
            ).wait_recv()

    for step, owner, to, cut in targets:
        itself = (to == t) & (cut == c)

        @pl.when(jnp.logical_not(itself))
        def _():
            copy(step, owner, to, cut).wait_send()


def dealt(plan, tiles):
    return pl.pallas_call(
        functools.partial(deal_kernel, plan),
        out_shape=jax.ShapeDtypeStruct((plan.fine, 2 * SUB, LANES), tiles.dtype),
        in_specs=[pl.BlockSpec(memory_space=pltpu.VMEM)],
        out_specs=pl.BlockSpec(memory_space=pltpu.VMEM),
        scratch_shapes=[
            pltpu.SemaphoreType.DMA((plan.times, plan.owners)),
            pltpu.SemaphoreType.DMA((plan.fine,)),
        ],
        compiler_params=pltpu.CompilerParams(collective_id=1, has_side_effects=True),
    )(tiles)


def order_of(plan):
    bins = F // plan.cuts
    order = np.zeros((plan.fine, 2, SUB, 2, bins), np.float32)
    for fine in range(plan.fine):
        for part in range(2):
            for i in range(plan.per_owner):
                order[fine, part, i, part, plan.fine * i + fine] = 1.0
    return order.reshape(plan.fine * 2 * SUB, 2 * bins).astype(jnp.bfloat16)


def settle_kernel(plan, tiles, order, out):
    rows = plan.fine * 2 * SUB
    wide = lax.dot_general(
        tiles[...].reshape(rows, LANES),
        order[...],
        (((0,), (0,)), ((), ())),
        preferred_element_type=jnp.float32,
    )
    bins = F // plan.cuts
    if plan.lags < LANES:
        pieces = LANES // plan.lags
        which = lax.axis_index("tm") % pieces
        kept = wide[: plan.lags]
        for piece in range(1, pieces):
            kept = jnp.where(
                which == piece, wide[piece * plan.lags : (piece + 1) * plan.lags], kept
            )
        wide = kept
    out[:, 0, :] = wide[:, :bins]
    out[:, 1, :] = wide[:, bins:]


def settled(plan, tiles):
    return pl.pallas_call(
        functools.partial(settle_kernel, plan),
        out_shape=jax.ShapeDtypeStruct((plan.lags, 2, F // plan.cuts), jnp.float32),
        in_specs=[pl.BlockSpec(memory_space=pltpu.VMEM)] * 2,
        out_specs=pl.BlockSpec(memory_space=pltpu.VMEM),
    )(tiles, jnp.asarray(order_of(plan)))


def paired_rows(x):
    samples = x.shape[1] * x.shape[2]
    split = x.reshape(2, samples // LANES, LANES).transpose(1, 0, 2)
    return split.reshape(2 * samples // LANES, LANES)


def on_device(surveillance, reference_signal):
    times, cuts = lax.axis_size("tm"), lax.axis_size("dop")
    samples = surveillance.shape[1] * surveillance.shape[2]
    plan = Plan(times, cuts, samples * times * cuts)
    me = lambda: lax.axis_index("tm") * cuts + lax.axis_index("dop")
    gs, gr = everywhere(plan, [paired_rows(surveillance), paired_rows(reference_signal)])
    gr = jnp.pad(gr, ((UNIT // 2, 0), (0, 0)))
    return settled(plan, dealt(plan, lag_maps(plan, me, gs, gr)))


def solution(mesh):
    return jax.shard_map(
        on_device,
        mesh=mesh,
        in_specs=(P(None, "tm", "dop"), P(None, "tm", "dop")),
        out_specs=P("tm", None, "dop"),
        check_vma=False,
    )
```

time: 69.2 us -> 50.8 us (0.73)
  local copies, waits for them, and re-layouts: 14.9 us -> 1.86 us
  other arithmetic: 3.06 us -> 0 us
  Pallas kernels: 50.3 us -> 48.1 us
    reshape x10 -> x0, local copies, waits for them, and re-layouts: 7.49 us -> none  [the longest x2 2.67 us: everywhere(): value.reshape(rows, 128)]
    convert_element_type x4 -> x0, local copies, waits for them, and re-layouts: 4.29 us -> none  [ambiguity_lags(): signal.reshape(2, depth, phases).transpose(0, 2, 1).astype(jnp.float32)]
    slice x2 -> x0, local copies, waits for them, and re-layouts: 2.6 us -> none  [the longest x1 1.46 us: ambiguity_lags(): near = delayed[:, :window].reshape(2, depth, phases)]
    pallas_call x3 -> x4, Pallas kernels: 50.3 us -> 48.1 us  [the longest x1 19.9 us: everywhere(): pl.pallas_call(functools.partial(spread_kernel, [order, other], plan.cuts...]
    pad x0 -> x1, local copies, waits for them, and re-layouts: none -> 1.86 us  [on_device(): gr = jnp.pad(gr, ((UNIT // 2, 0), (0, 0)))]
    convert_element_type x1 -> x0, other arithmetic: 1.58 us -> none  [ambiguity_lags(): jnp.concatenate([near, far], 2).transpose(0, 2, 1).astype(jnp.float32)]
    another operation x1 -> x0, other arithmetic: 1.08 us -> none  [ambiguity_lags(): jnp.stack([strided[0] * c - strided[1] * s, strided[1] * c + strided[0] *...]
where the time goes in v1:
time: 50.8 us; the launch traced here: 50 us
  Pallas kernels  48.1 us (95%)
  local copies, waits for them, and re-layouts  1.86 us (4%)
    pallas_call x1, Pallas kernels, everywhere(): pl.pallas_call(functools.partial(spread_kernel, [order, other], plan.cuts...  19.9 us
    pallas_call x1, Pallas kernels, lag_maps(): pl.pallas_call(functools.partial(compute_kernel, plan, me), out_shape=jax...  16.5 us
    pallas_call x1, Pallas kernels, dealt(): pl.pallas_call(functools.partial(deal_kernel, plan), out_shape=jax.ShapeD...  9.59 us
    pallas_call x1, Pallas kernels, settled(): pl.pallas_call(functools.partial(settle_kernel, plan), out_shape=jax.Shap...  2.12 us
    pad x1, local copies, waits for them, and re-layouts, on_device(): gr = jnp.pad(gr, ((UNIT // 2, 0), (0, 0)))  1.86 us

profile of v1, /device:TPU:1, one launch (start us, length us, event | category | flops | bytes accessed | tf_op | source)
XLA Modules:
  0.0 50.0 jit_solution(18102234135028519684)
XLA Ops:
  0.0 19.9 %shard_map.64 = (bf16[32,64,128]{2,1,0:T(8,128)(2,1)}, bf16[32,64,128]{2,1,0:T(8,128)(2,1)}) custom-call(bf16[64,128]{1,0:T(8,128)(2,1)} %bitcast.14, bf16[64,128]{1,0:T(8,128)(2,1)} %bitcast.15), custom_call_target="tpu_custom_call" | custom-call | tf_op jit(solution)/shard_map/pallas_call | solution.py:395
  19.9 1.9 %pad.4.gr = bf16[2080,128]{1,0:T(8,128)(2,1)} pad(bf16[2048,128]{1,0:T(8,128)(2,1)} %bitcast.13, bf16[]{:T(256)} %constant.10.clone.1), padding=32_0x0_0 | pad | bytes 1056770 | tf_op jit(solution)/shard_map/jit(_pad)/pad | solution.py:546
  21.8 16.5 %shard_map.65.tiles = bf16[16,2,16,128]{3,2,1,0:T(8,128)(2,1)} custom-call(bf16[2048,128]{1,0:T(8,128)(2,1)} %bitcast.12, bf16[2080,128]{1,0:T(8,128)(2,1)} %pad.4.gr, bf16[4,256,256]{2,1,0:T(8,128)(2,1)} %constant.11.clone.waves, f32[32,2,8,128]{3,2,1,0:T(8,128)} %constant.12.clone.forward, f32[32,2,8,128]{3,2,1,0:T(8,128)} %constant.13.clone.back), custom_call_target="tpu_custom_call" | custom-call | tf_op jit(solution)/shard_map/pallas_call | solution.py:301
  38.3 9.6 %shard_map.66.tiles = bf16[32,16,128]{2,1,0:T(8,128)(2,1)} custom-call(bf16[16,2,16,128]{3,2,1,0:T(8,128)(2,1)} %shard_map.65.tiles), custom_call_target="tpu_custom_call" | custom-call | tf_op jit(solution)/shard_map/pallas_call | solution.py:480
  47.9 2.1 %shard_map.67 = f32[128,2,256]{2,1,0:T(2,128)} custom-call(bf16[32,16,128]{2,1,0:T(8,128)(2,1)} %shard_map.66.tiles, bf16[512,512]{1,0:T(8,128)(2,1)} %constant.14.clone.order), custom_call_target="tpu_custom_call" | custom-call | tf_op jit(solution)/shard_map/pallas_call | solution.py:526

commit v2 on v1

--- a/solution.py
+++ b/solution.py
@@ -276,188 +276,147 @@
                 )
 
 
-def compute_kernel(plan, me, gs, gr, waves, forward, back, out, *scratch):
-    drift, even, odd, stage, stage2, high, low, S, R, yhigh, ylow, Z = scratch
-    me = me()
-    fine = me // plan.share
-    first = (me % plan.share) * plan.mine
-    prepare(plan, fine, drift, even, odd)
-
-    @pl.loop(0, plan.groups)
-    def _(group):
-        work = (drift, even, odd, stage, high, low)
-        signal_group(plan, group, gs, waves, forward, work, S)
-        reference_group(plan, group, gr, waves, forward, (stage, stage2, high, low), R)
-
-    cross_spectra(plan, first, S, R, yhigh, ylow)
-    to_lags(plan, waves, back, yhigh, ylow, Z, out)
-
-
-def lag_maps(plan, me, gs, gr, interpret=False):
-    waves, forward, back = tables(plan)
-    tall = plan.owners * SUB
-    reach = plan.shifts
-    f32, bf16 = jnp.float32, jnp.bfloat16
-    return pl.pallas_call(
-        functools.partial(compute_kernel, plan, me),
-        out_shape=jax.ShapeDtypeStruct((N1, plan.owners, 2 * SUB, LANES), bf16),
-        in_specs=[pl.BlockSpec(memory_space=pltpu.VMEM)] * 5,
-        out_specs=pl.BlockSpec(memory_space=pltpu.VMEM),
-        scratch_shapes=[
-            pltpu.VMEM((plan.groups, 2, SUB, LANES), f32),
-            pltpu.VMEM((N1, 2, SUB, LANES), f32),
-            pltpu.VMEM((N1, 2, SUB, LANES), f32),
-            pltpu.VMEM((4 * UNIT, LANES), f32),
-            pltpu.VMEM((4 * UNIT, LANES), f32),
-            pltpu.VMEM((F1 * SUB, 2 * LANES), bf16),
-            pltpu.VMEM((F1 * SUB, 2 * LANES), bf16),
-            pltpu.VMEM((F1 + reach, plan.groups, 2, SUB, LANES), f32),
-            pltpu.VMEM((F1, plan.groups, 2, SUB, LANES), f32),
-            pltpu.VMEM((F1 * tall, 2 * LANES), bf16),
-            pltpu.VMEM((F1 * tall, 2 * LANES), bf16),
-            pltpu.VMEM((F1 * tall, 2 * LANES), f32),
-        ],
-        compiler_params=pltpu.CompilerParams(vmem_limit_bytes=56 * 1024 * 1024),
-        interpret=interpret,
-    )(gs, gr, jnp.asarray(waves), jnp.asarray(forward), jnp.asarray(back))
-
-
-def flipped(index, bit):
-    weight = 1 << bit
-    return index + weight * (1 - 2 * ((index // weight) % 2))
-
-
-def spread_kernel(orders, cuts, *refs):
-    count = len(orders)
-    own, every = refs[:count], refs[count : 2 * count]
-    send_sems, recv_sems = refs[2 * count :]
-    me = lax.axis_index("tm") * cuts + lax.axis_index("dop")
-
-    def place(index):
-        return {"tm": index // cuts, "dop": index % cuts}
-
+def across(plan, own, every, sems, prepared):
+    send_sems, recv_sems = sems
+    cuts, far = plan.cuts, plan.times // 4
+    t, c = lax.axis_index("tm"), lax.axis_index("dop")
+    z, near = t // 4, t % 4
+    beside = (flipped(near, 0), flipped(near, 1))
+    others = [flipped_by(z, k) for k in range(1, far)]
+    fellows = [flipped_by(c, k) for k in range(1, cuts)]
+
+    partners = [(z * 4 + n, c) for n in beside]
+    partners += [(other * 4 + near, c) for other in others]
+    partners += [(t, fellow) for fellow in fellows]
     barrier = pltpu.get_barrier_semaphore()
-    for bit in orders[0]:
+    for to, cut in partners:
         pl.semaphore_signal(
-            barrier,
-            inc=1,
-            device_id=place(flipped(me, bit)),
-            device_id_type=pl.DeviceIdType.MESH,
+            barrier, inc=1, device_id={"tm": to, "dop": cut}, device_id_type=MESH
         )
-    pl.semaphore_wait(barrier, len(orders[0]))
-
-    def copy(which, source, block, slot, target):
+    pl.semaphore_wait(barrier, len(partners))
+
+    sent = []
+    rows = own[0].shape[0]
+    pad = (0, UNIT // 2)
+
+    def place(which, source):
+        start = pl.multiple_of(source * rows, rows) + pad[which]
+        return every[which].at[pl.ds(pl.multiple_of(start, 16), rows)]
+
+    def copy(which, source, src, to, cut, slot):
         return pltpu.make_async_remote_copy(
-            src_ref=source,
-            dst_ref=every[which].at[block],
-            send_sem=send_sems.at[which, slot],
-            recv_sem=recv_sems.at[which, block],
-            device_id=place(target),
-            device_id_type=pl.DeviceIdType.MESH,
+            src_ref=src,
+            dst_ref=place(which, source),
+            send_sem=send_sems.at[slot],
+            recv_sem=recv_sems.at[which, source],
+            device_id={"tm": to, "dop": cut},
+            device_id_type=MESH,
         )
 
-    sent = []
-    held = [[me] for _ in orders]
-    landed = [1] * count
-    for step in range(len(orders[0])):
-        partners = [flipped(me, order[step]) for order in orders]
-        for at in range(1 << step):
-            for which in range(count):
-                block = held[which][at]
-                mine = every[which].at[block]
-                if at == 0:
-                    mine = own[which]
-                elif at >= landed[which]:
-                    copy(which, mine, block, 0, partners[which]).wait_recv()
-                    landed[which] = at + 1
-                one = copy(which, mine, block, (1 << step) - 1 + at, partners[which])
-                one.start()
-                sent.append(one)
-        for which, order in enumerate(orders):
-            held[which] = held[which] + [flipped(h, order[step]) for h in held[which]]
-        if step == 0:
-            for which in range(count):
-                every[which][pl.ds(me, 1)] = own[which][...][None]
-    for which in range(count):
-        for at in range(landed[which], len(held[which])):
-            block = held[which][at]
-            copy(which, own[which], block, 0, flipped(me, 0)).wait_recv()
-    for one in sent:
-        one.wait_send()
-
-
-def everywhere(plan, values):
-    bits = plan.devices.bit_length() - 1
-    order = list(range(bits))[::-1]
-    other = order[:-3] + [order[-2], order[-3], order[-1]]
-    rows = values[0].shape[0]
-    block = jax.ShapeDtypeStruct((plan.devices, rows, LANES), values[0].dtype)
-    gathered = pl.pallas_call(
-        functools.partial(spread_kernel, [order, other], plan.cuts),
-        out_shape=[block] * 2,
-        in_specs=[pl.BlockSpec(memory_space=pltpu.VMEM)] * 2,
-        out_specs=[pl.BlockSpec(memory_space=pltpu.VMEM)] * 2,
-        scratch_shapes=[
-            pltpu.SemaphoreType.DMA((2, plan.devices)),
-            pltpu.SemaphoreType.DMA((2, plan.devices)),
-        ],
-        compiler_params=pltpu.CompilerParams(collective_id=0, has_side_effects=True),
-    )(*values)
-    return [every.reshape(plan.devices * rows, LANES) for every in gathered]
-
-
-def deal_kernel(plan, tiles, out, send_sems, recv_sems):
-    cuts, times = plan.cuts, plan.times
+    def send(which, source, to, cut, mine=False):
+        src = own[which] if mine else place(which, source)
+        one = copy(which, source, src, to, cut, len(sent))
+        one.start()
+        sent.append(one)
+
+    def landed(which, source):
+        copy(which, source, own[which], t, c, 0).wait_recv()
+
+    me = t * cuts + c
+    for other in others[::-1]:
+        for which in range(2):
+            send(which, me, other * 4 + near, c, True)
+    for n in beside:
+        for which in range(2):
+            send(which, me, z * 4 + n, c, True)
+    for fellow in fellows:
+        for which in range(2):
+            send(which, me, t, fellow, True)
+    for which in range(2):
+        every[which][pl.ds(pl.multiple_of(me * rows + pad[which], 16), rows)] = own[
+            which
+        ][...]
+    prepared()
+
+    corner = flipped(beside[0], 1)
+    levels = [z] + others
+    for k in range(far + 1):
+        if k < far:
+            level = levels[k]
+            if k > 0:
+                source = (level * 4 + near) * cuts + c
+                for which in range(2):
+                    landed(which, source)
+                    for n in beside:
+                        send(which, source, z * 4 + n, c)
+                    for fellow in fellows:
+                        send(which, source, t, fellow)
+            for side in range(2):
+                source = (level * 4 + beside[side]) * cuts + c
+                for which in range(2):
+                    landed(which, source)
+                    if which == side:
+                        send(which, source, z * 4 + beside[1 - side], c)
+                    for fellow in fellows:
+                        send(which, source, t, fellow)
+        if k > 0:
+            source = (levels[k - 1] * 4 + corner) * cuts + c
+            for which in range(2):
+                landed(which, source)
+                for fellow in fellows:
+                    send(which, source, t, fellow)
+    for fellow in fellows:
+        for level in levels:
+            for n in (near, beside[0], beside[1], corner):
+                for which in range(2):
+                    landed(which, (level * 4 + n) * cuts + fellow)
+    return sent
+
+
+def sends_needed(plan):
+    far, fellows = plan.times // 4, plan.cuts - 1
+    return 2 * (far - 1 + 2 + fellows) + 2 * (far - 1) * (2 + fellows) + (
+        far * (2 + 6 * fellows)
+    )
+
+
+def deal(plan, tiles, out, sems):
+    send_sems, recv_sems = sems
+    times = plan.times
     t, c = lax.axis_index("tm"), lax.axis_index("dop")
-    me = t * cuts + c
+    me = t * plan.cuts + c
     fine = me // plan.share
     base = (me % plan.share) * plan.owners
-    mine = c // plan.owners
-
-    barrier = pltpu.get_barrier_semaphore()
-    here = fine * 0
-    targets = []
-    for step in range(times):
-        to = (t + step) % times
-        for owner in range(plan.owners):
-            targets.append((step, owner, to, base + owner))
-    for step, owner, to, cut in targets:
-        itself = (to == t) & (cut == c)
-
-        @pl.when(jnp.logical_not(itself))
-        def _():
-            pl.semaphore_signal(
-                barrier, inc=1, device_id={"tm": to, "dop": cut}, device_id_type=MESH
-            )
-
-    sends_to_me = (base <= c) & (c < base + plan.owners)
-    expected = plan.fine - jnp.where(sends_to_me, 1, 0)
-    pl.semaphore_wait(barrier, expected)
-
-    def copy(step, owner, to, cut):
+    to_me = (base <= c) & (c < base + plan.owners)
+
+    def copy(step, owner):
+        to = flipped_by(t, step)
         return pltpu.make_async_remote_copy(
             src_ref=tiles.at[to * plan.lags // LANES, owner],
             dst_ref=out.at[fine],
             send_sem=send_sems.at[step, owner],
             recv_sem=recv_sems.at[fine],
-            device_id={"tm": to, "dop": cut},
+            device_id={"tm": to, "dop": base + owner},
             device_id_type=MESH,
         )
 
-    for step, owner, to, cut in targets:
-        itself = (to == t) & (cut == c)
+    for step in range(times - 1, 0, -1):
+        for owner in range(plan.owners):
+            copy(step, owner).start()
+    for owner in range(plan.owners):
+        itself = base + owner == c
 
         @pl.when(jnp.logical_not(itself))
         def _():
-            copy(step, owner, to, cut).start()
+            copy(0, owner).start()
 
         @pl.when(itself)
         def _():
-            out[fine] = tiles[to * plan.lags // LANES, owner]
+            out[fine] = tiles[t * plan.lags // LANES, owner]
 
     for source in range(plan.fine):
 
-        @pl.when((fine != source) | jnp.logical_not(sends_to_me))
+        @pl.when((fine != source) | jnp.logical_not(to_me))
         def _():
             pltpu.make_async_remote_copy(
                 src_ref=tiles.at[0, 0],
@@ -468,26 +427,107 @@
                 device_id_type=MESH,
             ).wait_recv()
 
-    for step, owner, to, cut in targets:
-        itself = (to == t) & (cut == c)
-
-        @pl.when(jnp.logical_not(itself))
+    for step in range(1, times):
+        for owner in range(plan.owners):
+            copy(step, owner).wait_send()
+    for owner in range(plan.owners):
+
+        @pl.when(base + owner != c)
         def _():
-            copy(step, owner, to, cut).wait_send()
-
-
-def dealt(plan, tiles):
+            copy(0, owner).wait_send()
+
+
+def whole_kernel(plan, s, r, waves_at, forward_at, back_at, out, *scratch):
+    (gs, gr, waves, forward, back, tiles) = scratch[:6]
+    drift, even, odd, stage, stage2, high, low, S, R, yhigh, ylow, Z = scratch[6:18]
+    load_sems, gather_sems, deal_sems = scratch[18], scratch[19:21], scratch[21:23]
+    me = lax.axis_index("tm") * plan.cuts + lax.axis_index("dop")
+    fine = me // plan.share
+    first = (me % plan.share) * plan.mine
+    loads = [
+        pltpu.make_async_copy(source, target, load_sems.at[i])
+        for i, (source, target) in enumerate(
+            ((waves_at, waves), (forward_at, forward), (back_at, back))
+        )
+    ]
+
+    def prepared():
+        for load in loads:
+            load.start()
+        gr[: UNIT // 2, :] = jnp.zeros((UNIT // 2, LANES), jnp.bfloat16)
+        prepare(plan, fine, drift, even, odd)
+
+    sent = across(plan, (s, r), (gs, gr), gather_sems, prepared)
+    for load in loads:
+        load.wait()
+
+    @pl.loop(0, plan.groups)
+    def _(group):
+        work = (drift, even, odd, stage, high, low)
+        signal_group(plan, group, gs, waves, forward, work, S)
+        reference_group(plan, group, gr, waves, forward, (stage, stage2, high, low), R)
+
+    cross_spectra(plan, first, S, R, yhigh, ylow)
+    to_lags(plan, waves, back, yhigh, ylow, Z, tiles)
+    deal(plan, tiles, out, deal_sems)
+    for one in sent:
+        one.wait_send()
+
+
+def dealt_maps(plan, s, r):
+    waves, forward, back = tables(plan)
+    tall = plan.owners * SUB
+    f32, bf16 = jnp.float32, jnp.bfloat16
+    samples = 2 * plan.window // LANES
     return pl.pallas_call(
-        functools.partial(deal_kernel, plan),
-        out_shape=jax.ShapeDtypeStruct((plan.fine, 2 * SUB, LANES), tiles.dtype),
-        in_specs=[pl.BlockSpec(memory_space=pltpu.VMEM)],
+        functools.partial(whole_kernel, plan),
+        out_shape=jax.ShapeDtypeStruct((plan.fine, 2 * SUB, LANES), bf16),
+        in_specs=[pl.BlockSpec(memory_space=pltpu.VMEM)] * 2
+        + [pl.BlockSpec(memory_space=pl.ANY)] * 3,
         out_specs=pl.BlockSpec(memory_space=pltpu.VMEM),
         scratch_shapes=[
+            pltpu.VMEM((samples, LANES), bf16),
+            pltpu.VMEM((samples + UNIT // 2, LANES), bf16),
+            pltpu.VMEM(waves.shape, bf16),
+            pltpu.VMEM(forward.shape, f32),
+            pltpu.VMEM(back.shape, f32),
+            pltpu.VMEM((N1, plan.owners, 2 * SUB, LANES), bf16),
+            pltpu.VMEM((plan.groups, 2, SUB, LANES), f32),
+            pltpu.VMEM((N1, 2, SUB, LANES), f32),
+            pltpu.VMEM((N1, 2, SUB, LANES), f32),
+            pltpu.VMEM((4 * UNIT, LANES), f32),
+            pltpu.VMEM((4 * UNIT, LANES), f32),
+            pltpu.VMEM((F1 * SUB, 2 * LANES), bf16),
+            pltpu.VMEM((F1 * SUB, 2 * LANES), bf16),
+            pltpu.VMEM((F1 + plan.shifts, plan.groups, 2, SUB, LANES), f32),
+            pltpu.VMEM((F1, plan.groups, 2, SUB, LANES), f32),
+            pltpu.VMEM((F1 * tall, 2 * LANES), bf16),
+            pltpu.VMEM((F1 * tall, 2 * LANES), bf16),
+            pltpu.VMEM((F1 * tall, 2 * LANES), f32),
+            pltpu.SemaphoreType.DMA((3,)),
+            pltpu.SemaphoreType.DMA((sends_needed(plan),)),
+            pltpu.SemaphoreType.DMA((2, plan.devices)),
             pltpu.SemaphoreType.DMA((plan.times, plan.owners)),
             pltpu.SemaphoreType.DMA((plan.fine,)),
         ],
-        compiler_params=pltpu.CompilerParams(collective_id=1, has_side_effects=True),
-    )(tiles)
+        compiler_params=pltpu.CompilerParams(
+            collective_id=0,
+            has_side_effects=True,
+            vmem_limit_bytes=56 * 1024 * 1024,
+        ),
+    )(s, r, jnp.asarray(waves), jnp.asarray(forward), jnp.asarray(back))
+
+
+def flipped(index, bit):
+    weight = 1 << bit
+    return index + weight * (1 - 2 * ((index // weight) % 2))
+
+
+def flipped_by(index, mask):
+    for bit in range(mask.bit_length()):
+        if mask >> bit & 1:
+            index = flipped(index, bit)
+    return index
 
 
 def order_of(plan):
@@ -541,10 +581,8 @@
     times, cuts = lax.axis_size("tm"), lax.axis_size("dop")
     samples = surveillance.shape[1] * surveillance.shape[2]
     plan = Plan(times, cuts, samples * times * cuts)
-    me = lambda: lax.axis_index("tm") * cuts + lax.axis_index("dop")
-    gs, gr = everywhere(plan, [paired_rows(surveillance), paired_rows(reference_signal)])
-    gr = jnp.pad(gr, ((UNIT // 2, 0), (0, 0)))
-    return settled(plan, dealt(plan, lag_maps(plan, me, gs, gr)))
+    tiles = dealt_maps(plan, paired_rows(surveillance), paired_rows(reference_signal))
+    return settled(plan, tiles)
 
 
 def solution(mesh):

time: 50.8 us -> 45.8 us (0.902)
  Pallas kernels: 48.1 us -> 45.1 us
  local copies, waits for them, and re-layouts: 1.86 us -> 0 us
    pallas_call x3 -> x1, Pallas kernels: 46 us -> 42.9 us  [dealt_maps(): pl.pallas_call(functools.partial(whole_kernel, plan), out_shape=jax.Shape...]
    pad x1 -> x0, local copies, waits for them, and re-layouts: 1.86 us -> none  [on_device(): gr = jnp.pad(gr, ((UNIT // 2, 0), (0, 0)))]
where the time goes in v2:
time: 45.8 us; the launch traced here: 45.1 us
  Pallas kernels  45.1 us (98%)
    pallas_call x1, Pallas kernels, dealt_maps(): pl.pallas_call(functools.partial(whole_kernel, plan), out_shape=jax.Shape...  42.9 us
    pallas_call x1, Pallas kernels, settled(): pl.pallas_call(functools.partial(settle_kernel, plan), out_shape=jax.Shap...  2.12 us

profile of v2, /device:TPU:1, one launch (start us, length us, event | category | flops | bytes accessed | tf_op | source)
XLA Modules:
  0.0 45.1 jit_solution(11033959421345356718)
XLA Ops:
  0.0 42.9 %shard_map.64.tiles = bf16[32,16,128]{2,1,0:T(8,128)(2,1)} custom-call(bf16[64,128]{1,0:T(8,128)(2,1)} %bitcast.10, bf16[64,128]{1,0:T(8,128)(2,1)} %bitcast.11, bf16[4,256,256]{2,1,0:T(8,128)(2,1)} %constant.8.clone.waves_at, f32[32,2,8,128]{3,2,1,0:T(8,128)} %constant.9.clone.forward_at, f32[32,2,8,128]{3,2,1,0:T(8,128)} %constant.10.clone.back_at), custom_call_target="tpu_custom_call" | custom-call | tf_op jit(solution)/shard_map/pallas_call | solution.py:482
  43.0 2.1 %shard_map.65 = f32[128,2,256]{2,1,0:T(2,128)} custom-call(bf16[32,16,128]{2,1,0:T(8,128)(2,1)} %shard_map.64.tiles, bf16[512,512]{1,0:T(8,128)(2,1)} %constant.11.clone.order), custom_call_target="tpu_custom_call" | custom-call | tf_op jit(solution)/shard_map/pallas_call | solution.py:566

commit v3 on v2

--- a/solution.py
+++ b/solution.py
@@ -16,7 +16,9 @@
 POINTS = 2 * LAGS
 N1 = LAGS // LANES
 F1 = POINTS // LANES
-UNIT = 2 * N1 * 2
+ROWS = 2 * N1
+GROUP = SUB * ROWS
+APART = ROWS + 1
 MESH = pl.DeviceIdType.MESH
 
 
@@ -24,8 +26,8 @@
     def __init__(self, times, cuts, window):
         self.times, self.cuts, self.window = times, cuts, window
         self.devices = times * cuts
-        self.units = window // (2 * LAGS)
-        self.groups = self.units // 4
+        self.groups = window // (SUB * LAGS)
+        self.far = times // 4
         self.fine = window // POINTS
         self.shifts = F // self.fine
         self.share = self.devices // self.fine
@@ -119,7 +121,7 @@
 
     @pl.loop(0, plan.groups)
     def _(group):
-        segment = 2 * ((sub // 2) * plan.groups + group) + sub % 2
+        segment = SUB * group + sub
         c, s = phases_of(fine * (lane + segment * LAGS), plan.window)
         drift[group, 0] = c
         drift[group, 1] = s
@@ -135,9 +137,20 @@
         odd[row, 1] = s
 
 
-def spread_rows(stage):
+def staged(rows, stage):
+    for i in range(rows.shape[0] // ROWS):
+        stage[i * APART : i * APART + ROWS, :] = rows[
+            i * ROWS : (i + 1) * ROWS, :
+        ].astype(jnp.float32)
+
+
+def spread_rows(stage, skip=0):
+    first = skip * APART
     return [
-        tuple(stage[pl.ds(2 * n + part, SUB, stride=2 * N1), :] for part in range(2))
+        tuple(
+            stage[pl.ds(first + 2 * n + part, SUB, stride=APART), :]
+            for part in range(2)
+        )
         for n in range(N1)
     ]
 
@@ -164,13 +177,10 @@
     )
 
 
-def signal_group(plan, group, gs, waves, forward, work, S):
+def signal_group(plan, group, slot, gs, waves, forward, work, S):
     drift, even, odd, stage, high, low = work
-    for z in range(4):
-        start = pl.multiple_of((z * plan.groups + group) * UNIT, UNIT)
-        stage[z * UNIT : (z + 1) * UNIT, :] = gs[pl.ds(start, UNIT), :].astype(
-            jnp.float32
-        )
+    start = pl.multiple_of(group * GROUP, GROUP)
+    staged(gs[pl.ds(start, GROUP), :], stage)
     here = (drift[group, 0], drift[group, 1])
     x = [times_(v, here) for v in spread_rows(stage)]
     for parity, table in enumerate((even, odd)):
@@ -182,21 +192,18 @@
         row = (f1 % 2) * 128 + (f1 // 2) * SUB
         for part in range(2):
             v = wide[row : row + SUB, part * LANES : (part + 1) * LANES]
-            S[reach + f1, group, part] = v
+            S[slot, reach + f1, part] = v
             if f1 < reach:
-                S[reach + f1 + F1, group, part] = pltpu.roll(v, LANES - 1, 1)
+                S[slot, reach + f1 + F1, part] = pltpu.roll(v, LANES - 1, 1)
             if f1 >= F1 - reach:
-                S[reach + f1 - F1, group, part] = pltpu.roll(v, 1, 1)
-
-
-def reference_group(plan, group, gr, waves, forward, work, R):
-    stage, stage2, high, low = work
-    for z in range(4):
-        start = pl.multiple_of((z * plan.groups + group) * UNIT, UNIT)
-        rows = slice(z * UNIT, (z + 1) * UNIT)
-        stage2[rows, :] = gr[pl.ds(start, UNIT), :].astype(jnp.float32)
-        stage[rows, :] = gr[pl.ds(start + UNIT // 2, UNIT), :].astype(jnp.float32)
-    now, before = spread_rows(stage), spread_rows(stage2)
+                S[slot, reach + f1 - F1, part] = pltpu.roll(v, 1, 1)
+
+
+def reference_group(plan, group, slot, gr, waves, forward, work, R):
+    stage, high, low = work
+    start = pl.multiple_of(group * GROUP, GROUP)
+    staged(gr[pl.ds(start, GROUP + ROWS), :], stage)
+    before, now = spread_rows(stage), spread_rows(stage, 1)
     y = [plus(a, b) for a, b in zip(now, before)]
     turn_and_split(dft16(y, -1), 0, forward, high, low)
     y = [turned(minus(a, b), n, F1, -1) for n, (a, b) in enumerate(zip(now, before))]
@@ -205,7 +212,7 @@
     for f1 in range(F1):
         row = (f1 % 2) * 128 + (f1 // 2) * SUB
         for part in range(2):
-            R[f1, group, part] = wide[
+            R[slot, f1, part] = wide[
                 row : row + SUB, part * LANES : (part + 1) * LANES
             ]
 
@@ -223,29 +230,50 @@
     return values[0]
 
 
-def cross_spectra(plan, first, S, R, high, low):
+def product(plan, first, f1, owner, i, slots, S, R, held, start):
+    at = f1 + first + owner * plan.per_owner + i
+    index = owner * plan.per_owner + i
+    a = b = None
+    if not start:
+        a, b = held[f1, index, 0], held[f1, index, 1]
+    for slot in range(slots):
+        sr, si = S[slot, at, 0], S[slot, at, 1]
+        rr, ri = R[slot, f1, 0], R[slot, f1, 1]
+        u = sr * rr + si * ri
+        v = si * rr - sr * ri
+        a, b = (u, v) if a is None else (a + u, b + v)
+    return a, b
+
+
+def add_spectra(plan, first, slots, S, R, held, start):
+    step = 4
+
+    @pl.loop(0, F1 // step)
+    def _(block):
+        for k in range(step):
+            f1 = block * step + k
+            for owner in range(plan.owners):
+                for i in range(plan.per_owner):
+                    a, b = product(plan, first, f1, owner, i, slots, S, R, held, start)
+                    index = owner * plan.per_owner + i
+                    held[f1, index, 0] = a
+                    held[f1, index, 1] = b
+
+
+def last_spectra(plan, first, slots, S, R, held, high, low):
     @pl.loop(0, F1)
     def _(f1):
-        rr = [R[f1, g, 0] for g in range(plan.groups)]
-        ri = [R[f1, g, 1] for g in range(plan.groups)]
         blocks = []
         for owner in range(plan.owners):
-            re, im = [], []
+            found = []
             for i in range(SUB):
-                if i >= plan.per_owner:
-                    re.append(jnp.zeros((SUB, LANES), jnp.float32))
-                    im.append(jnp.zeros((SUB, LANES), jnp.float32))
-                    continue
-                at = f1 + first + owner * plan.per_owner + i
-                a = b = None
-                for g in range(plan.groups):
-                    sr, si = S[at, g, 0], S[at, g, 1]
-                    u = sr * rr[g] + si * ri[g]
-                    v = si * rr[g] - sr * ri[g]
-                    a, b = (u, v) if a is None else (a + u, b + v)
-                re.append(a)
-                im.append(b)
-            blocks.append((fold_rows(re), fold_rows(im)))
+                if i < plan.per_owner:
+                    found.append(
+                        product(plan, first, f1, owner, i, slots, S, R, held, False)
+                    )
+                else:
+                    found.append((jnp.zeros((SUB, LANES), jnp.float32),) * 2)
+            blocks.append([fold_rows([v[part] for v in found]) for part in range(2)])
         tall = plan.owners * SUB
         rows = pl.ds(pl.multiple_of(f1 * tall, tall), tall)
         for part in range(2):
@@ -276,17 +304,35 @@
                 )
 
 
-def across(plan, own, every, sems, prepared):
+def schedule(plan):
+    far = plan.far
+    orders, counts = [], []
+    for z in range(far):
+        here, order, count = set(), [], []
+        for k in range(far):
+            here.add(z ^ k)
+            for plane in range(far):
+                for half in range(2):
+                    ready = plane in here and (half or plane == 0 or plane - 1 in here)
+                    if ready and 2 * plane + half not in order:
+                        order.append(2 * plane + half)
+            count.append(len(order))
+        orders.append(order)
+        counts.append(count)
+    return orders, [min(c[k] for c in counts) for k in range(far)]
+
+
+def gather_and_compute(plan, own, every, sems, prepared, compute):
     send_sems, recv_sems = sems
-    cuts, far = plan.cuts, plan.times // 4
+    cuts, far = plan.cuts, plan.far
     t, c = lax.axis_index("tm"), lax.axis_index("dop")
     z, near = t // 4, t % 4
-    beside = (flipped(near, 0), flipped(near, 1))
-    others = [flipped_by(z, k) for k in range(1, far)]
+    beside = [flipped_by(near, k) for k in (1, 2, 3)]
+    levels = [flipped_by(z, k) for k in range(far)]
     fellows = [flipped_by(c, k) for k in range(1, cuts)]
 
     partners = [(z * 4 + n, c) for n in beside]
-    partners += [(other * 4 + near, c) for other in others]
+    partners += [(other * 4 + near, c) for other in levels[1:]]
     partners += [(t, fellow) for fellow in fellows]
     barrier = pltpu.get_barrier_semaphore()
     for to, cut in partners:
@@ -297,7 +343,7 @@
 
     sent = []
     rows = own[0].shape[0]
-    pad = (0, UNIT // 2)
+    pad = (0, ROWS)
 
     def place(which, source):
         start = pl.multiple_of(source * rows, rows) + pad[which]
@@ -313,71 +359,78 @@
             device_id_type=MESH,
         )
 
-    def send(which, source, to, cut, mine=False):
-        src = own[which] if mine else place(which, source)
-        one = copy(which, source, src, to, cut, len(sent))
-        one.start()
-        sent.append(one)
-
-    def landed(which, source):
-        copy(which, source, own[which], t, c, 0).wait_recv()
+    def send(source, to, cut, mine=False):
+        for which in range(2):
+            src = own[which] if mine else place(which, source)
+            one = copy(which, source, src, to, cut, len(sent))
+            one.start()
+            sent.append(one)
+
+    def landed(source):
+        for which in range(2):
+            copy(which, source, own[which], t, c, 0).wait_recv()
+
+    def pass_on(k):
+        for n in beside:
+            source = (levels[k] * 4 + n) * cuts + c
+            landed(source)
+            for fellow in fellows:
+                send(source, t, fellow)
+
+    def complete(k):
+        for fellow in fellows:
+            for n in [near] + beside:
+                landed((levels[k] * 4 + n) * cuts + fellow)
 
     me = t * cuts + c
-    for other in others[::-1]:
-        for which in range(2):
-            send(which, me, other * 4 + near, c, True)
+    for level in levels[:0:-1]:
+        send(me, level * 4 + near, c, True)
     for n in beside:
-        for which in range(2):
-            send(which, me, z * 4 + n, c, True)
+        send(me, z * 4 + n, c, True)
     for fellow in fellows:
-        for which in range(2):
-            send(which, me, t, fellow, True)
+        send(me, t, fellow, True)
     for which in range(2):
         every[which][pl.ds(pl.multiple_of(me * rows + pad[which], 16), rows)] = own[
             which
         ][...]
     prepared()
 
-    corner = flipped(beside[0], 1)
-    levels = [z] + others
-    for k in range(far + 1):
-        if k < far:
-            level = levels[k]
-            if k > 0:
-                source = (level * 4 + near) * cuts + c
-                for which in range(2):
-                    landed(which, source)
-                    for n in beside:
-                        send(which, source, z * 4 + n, c)
-                    for fellow in fellows:
-                        send(which, source, t, fellow)
-            for side in range(2):
-                source = (level * 4 + beside[side]) * cuts + c
-                for which in range(2):
-                    landed(which, source)
-                    if which == side:
-                        send(which, source, z * 4 + beside[1 - side], c)
-                    for fellow in fellows:
-                        send(which, source, t, fellow)
-        if k > 0:
-            source = (levels[k - 1] * 4 + corner) * cuts + c
-            for which in range(2):
-                landed(which, source)
-                for fellow in fellows:
-                    send(which, source, t, fellow)
-    for fellow in fellows:
-        for level in levels:
-            for n in (near, beside[0], beside[1], corner):
-                for which in range(2):
-                    landed(which, (level * 4 + n) * cuts + fellow)
+    pass_on(0)
+    for level in levels[1:]:
+        source = (level * 4 + near) * cuts + c
+        landed(source)
+        for n in beside:
+            send(source, z * 4 + n, c)
+        for fellow in fellows:
+            send(source, t, fellow)
+    orders, counts = schedule(plan)
+
+    def group_at(i):
+        group = orders[0][i] + 0 * z
+        for other in range(1, far):
+            group = jnp.where(z == other, orders[other][i], group)
+        return group
+
+    done = 0
+    for k in range(far):
+        complete(k)
+        whole = [group_at(i) for i in range(done, counts[k])]
+        if k == far - 1:
+            compute(whole, done == 0, True)
+            break
+        for group in whole[:-1]:
+            compute([group], done == 0, False)
+            done += 1
+        pass_on(k + 1)
+        for group in whole[-1:]:
+            compute([group], done == 0, False)
+            done += 1
     return sent
 
 
 def sends_needed(plan):
-    far, fellows = plan.times // 4, plan.cuts - 1
-    return 2 * (far - 1 + 2 + fellows) + 2 * (far - 1) * (2 + fellows) + (
-        far * (2 + 6 * fellows)
-    )
+    far, fellows = plan.far, plan.cuts - 1
+    return 2 * ((far - 1) + far * (3 + 4 * fellows))
 
 
 def deal(plan, tiles, out, sems):
@@ -439,8 +492,10 @@
 
 def whole_kernel(plan, s, r, waves_at, forward_at, back_at, out, *scratch):
     (gs, gr, waves, forward, back, tiles) = scratch[:6]
-    drift, even, odd, stage, stage2, high, low, S, R, yhigh, ylow, Z = scratch[6:18]
-    load_sems, gather_sems, deal_sems = scratch[18], scratch[19:21], scratch[21:23]
+    drift, even, odd, held = scratch[6:10]
+    stage, high, low, rstage, rhigh, rlow = scratch[10:16]
+    S, R, yhigh, ylow, Z = scratch[16:21]
+    load_sems, gather_sems, deal_sems = scratch[21], scratch[22:24], scratch[24:26]
     me = lax.axis_index("tm") * plan.cuts + lax.axis_index("dop")
     fine = me // plan.share
     first = (me % plan.share) * plan.mine
@@ -454,20 +509,24 @@
     def prepared():
         for load in loads:
             load.start()
-        gr[: UNIT // 2, :] = jnp.zeros((UNIT // 2, LANES), jnp.bfloat16)
+        gr[:ROWS, :] = jnp.zeros((ROWS, LANES), jnp.bfloat16)
         prepare(plan, fine, drift, even, odd)
-
-    sent = across(plan, (s, r), (gs, gr), gather_sems, prepared)
-    for load in loads:
-        load.wait()
-
-    @pl.loop(0, plan.groups)
-    def _(group):
-        work = (drift, even, odd, stage, high, low)
-        signal_group(plan, group, gs, waves, forward, work, S)
-        reference_group(plan, group, gr, waves, forward, (stage, stage2, high, low), R)
-
-    cross_spectra(plan, first, S, R, yhigh, ylow)
+        for load in loads:
+            load.wait()
+
+    def compute(groups, start, last):
+        for slot, group in enumerate(groups):
+            work = (drift, even, odd, stage, high, low)
+            signal_group(plan, group, slot, gs, waves, forward, work, S)
+            reference_group(
+                plan, group, slot, gr, waves, forward, (rstage, rhigh, rlow), R
+            )
+        if last:
+            last_spectra(plan, first, len(groups), S, R, held, yhigh, ylow)
+        else:
+            add_spectra(plan, first, len(groups), S, R, held, start)
+
+    sent = gather_and_compute(plan, (s, r), (gs, gr), gather_sems, prepared, compute)
     to_lags(plan, waves, back, yhigh, ylow, Z, tiles)
     deal(plan, tiles, out, deal_sems)
     for one in sent:
@@ -479,6 +538,8 @@
     tall = plan.owners * SUB
     f32, bf16 = jnp.float32, jnp.bfloat16
     samples = 2 * plan.window // LANES
+    counts = schedule(plan)[1]
+    slots = counts[-1] - counts[-2]
     return pl.pallas_call(
         functools.partial(whole_kernel, plan),
         out_shape=jax.ShapeDtypeStruct((plan.fine, 2 * SUB, LANES), bf16),
@@ -487,7 +548,7 @@
         out_specs=pl.BlockSpec(memory_space=pltpu.VMEM),
         scratch_shapes=[
             pltpu.VMEM((samples, LANES), bf16),
-            pltpu.VMEM((samples + UNIT // 2, LANES), bf16),
+            pltpu.VMEM((samples + ROWS, LANES), bf16),
             pltpu.VMEM(waves.shape, bf16),
             pltpu.VMEM(forward.shape, f32),
             pltpu.VMEM(back.shape, f32),
@@ -495,12 +556,15 @@
             pltpu.VMEM((plan.groups, 2, SUB, LANES), f32),
             pltpu.VMEM((N1, 2, SUB, LANES), f32),
             pltpu.VMEM((N1, 2, SUB, LANES), f32),
-            pltpu.VMEM((4 * UNIT, LANES), f32),
-            pltpu.VMEM((4 * UNIT, LANES), f32),
+            pltpu.VMEM((F1, plan.mine, 2, SUB, LANES), f32),
+            pltpu.VMEM((SUB * APART + 7, LANES), f32),
             pltpu.VMEM((F1 * SUB, 2 * LANES), bf16),
             pltpu.VMEM((F1 * SUB, 2 * LANES), bf16),
-            pltpu.VMEM((F1 + plan.shifts, plan.groups, 2, SUB, LANES), f32),
-            pltpu.VMEM((F1, plan.groups, 2, SUB, LANES), f32),
+            pltpu.VMEM((SUB * APART + APART + 7, LANES), f32),
+            pltpu.VMEM((F1 * SUB, 2 * LANES), bf16),
+            pltpu.VMEM((F1 * SUB, 2 * LANES), bf16),
+            pltpu.VMEM((slots, F1 + plan.shifts, 2, SUB, LANES), f32),
+            pltpu.VMEM((slots, F1, 2, SUB, LANES), f32),
             pltpu.VMEM((F1 * tall, 2 * LANES), bf16),
             pltpu.VMEM((F1 * tall, 2 * LANES), bf16),
             pltpu.VMEM((F1 * tall, 2 * LANES), f32),

time: 45.8 us -> 36 us (0.79)
  Pallas kernels: 45.1 us -> 35.2 us
    pallas_call x1, Pallas kernels: 42.9 us -> 33.1 us  [dealt_maps(): pl.pallas_call(functools.partial(whole_kernel, plan), out_shape=jax.Shape...]
where the time goes in v3:
time: 36 us; the launch traced here: 35.3 us
  Pallas kernels  35.2 us (98%)
    pallas_call x1, Pallas kernels, dealt_maps(): pl.pallas_call(functools.partial(whole_kernel, plan), out_shape=jax.Shape...  33.1 us
    pallas_call x1, Pallas kernels, settled(): pl.pallas_call(functools.partial(settle_kernel, plan), out_shape=jax.Shap...  2.12 us

profile of v3, /device:TPU:1, one launch (start us, length us, event | category | flops | bytes accessed | tf_op | source)
XLA Modules:
  0.0 35.3 jit_solution(5042632559672396425)
XLA Ops:
  0.0 33.1 %shard_map.64.tiles = bf16[32,16,128]{2,1,0:T(8,128)(2,1)} custom-call(bf16[64,128]{1,0:T(8,128)(2,1)} %bitcast.10, bf16[64,128]{1,0:T(8,128)(2,1)} %bitcast.11, bf16[4,256,256]{2,1,0:T(8,128)(2,1)} %constant.8.clone.waves_at, f32[32,2,8,128]{3,2,1,0:T(8,128)} %constant.9.clone.forward_at, f32[32,2,8,128]{3,2,1,0:T(8,128)} %constant.10.clone.back_at), custom_call_target="tpu_custom_call" | custom-call | tf_op jit(solution)/shard_map/pallas_call | solution.py:543
  33.1 2.1 %shard_map.65 = f32[128,2,256]{2,1,0:T(2,128)} custom-call(bf16[32,16,128]{2,1,0:T(8,128)(2,1)} %shard_map.64.tiles, bf16[512,512]{1,0:T(8,128)(2,1)} %constant.11.clone.order), custom_call_target="tpu_custom_call" | custom-call | tf_op jit(solution)/shard_map/pallas_call | solution.py:630

commit v4 on v3

--- a/solution.py
+++ b/solution.py
@@ -20,6 +20,7 @@
 GROUP = SUB * ROWS
 APART = ROWS + 1
 MESH = pl.DeviceIdType.MESH
+SIGNAL, REFER, HELD = 0, 6, 12
 
 
 class Plan:
@@ -137,11 +138,10 @@
         odd[row, 1] = s
 
 
-def staged(rows, stage):
+def staged(rows, stage, skip=0):
     for i in range(rows.shape[0] // ROWS):
-        stage[i * APART : i * APART + ROWS, :] = rows[
-            i * ROWS : (i + 1) * ROWS, :
-        ].astype(jnp.float32)
+        at = (i + skip) * APART
+        stage[at : at + ROWS, :] = rows[i * ROWS : (i + 1) * ROWS, :].astype(jnp.float32)
 
 
 def spread_rows(stage, skip=0):
@@ -177,8 +177,9 @@
     )
 
 
-def signal_group(plan, group, slot, gs, waves, forward, work, S):
+def signal_group(plan, group, slot, gs, waves, forward, work, A):
     drift, even, odd, stage, high, low = work
+    stage, high, low = stage.at[slot], high.at[slot], low.at[slot]
     start = pl.multiple_of(group * GROUP, GROUP)
     staged(gs[pl.ds(start, GROUP), :], stage)
     here = (drift[group, 0], drift[group, 1])
@@ -190,19 +191,28 @@
     reach = plan.shifts // 2
     for f1 in range(F1):
         row = (f1 % 2) * 128 + (f1 // 2) * SUB
-        for part in range(2):
-            v = wide[row : row + SUB, part * LANES : (part + 1) * LANES]
-            S[slot, reach + f1, part] = v
+        re = wide[row : row + SUB, :LANES]
+        im = wide[row : row + SUB, LANES:]
+        for k, v in enumerate((re + im, re, im)):
+            A[reach + f1, SIGNAL + 3 * slot + k] = v
             if f1 < reach:
-                S[slot, reach + f1 + F1, part] = pltpu.roll(v, LANES - 1, 1)
+                A[reach + f1 + F1, SIGNAL + 3 * slot + k] = pltpu.roll(
+                    v, LANES - 1, 1
+                )
             if f1 >= F1 - reach:
-                S[slot, reach + f1 - F1, part] = pltpu.roll(v, 1, 1)
-
-
-def reference_group(plan, group, slot, gr, waves, forward, work, R):
+                A[reach + f1 - F1, SIGNAL + 3 * slot + k] = pltpu.roll(v, 1, 1)
+
+
+def reference_group(plan, group, slot, gr, before, waves, forward, work, A):
     stage, high, low = work
+    stage, high, low = stage.at[slot], high.at[slot], low.at[slot]
     start = pl.multiple_of(group * GROUP, GROUP)
-    staged(gr[pl.ds(start, GROUP + ROWS), :], stage)
+    if before is None:
+        staged(gr[pl.ds(start, GROUP + ROWS), :], stage)
+    else:
+        staged(before[...], stage)
+        own = pl.multiple_of(start + ROWS, ROWS)
+        staged(gr[pl.ds(own, GROUP), :], stage, 1)
     before, now = spread_rows(stage), spread_rows(stage, 1)
     y = [plus(a, b) for a, b in zip(now, before)]
     turn_and_split(dft16(y, -1), 0, forward, high, low)
@@ -211,76 +221,65 @@
     wide = lanes_turned(high, low, waves, 0)
     for f1 in range(F1):
         row = (f1 % 2) * 128 + (f1 // 2) * SUB
-        for part in range(2):
-            R[slot, f1, part] = wide[
-                row : row + SUB, part * LANES : (part + 1) * LANES
-            ]
-
-
-def fold_rows(values):
-    sub = lax.broadcasted_iota(jnp.int32, (SUB, LANES), 0)
-    step = 1
-    while step < SUB:
-        upper = (sub // step) % 2 == 1
-        values = [
-            jnp.where(upper, b, a) + pltpu.roll(jnp.where(upper, a, b), step, 0)
-            for a, b in zip(values[::2], values[1::2])
-        ]
-        step *= 2
-    return values[0]
-
-
-def product(plan, first, f1, owner, i, slots, S, R, held, start):
-    at = f1 + first + owner * plan.per_owner + i
-    index = owner * plan.per_owner + i
-    a = b = None
-    if not start:
-        a, b = held[f1, index, 0], held[f1, index, 1]
+        re = wide[row : row + SUB, :LANES]
+        im = wide[row : row + SUB, LANES:]
+        for k, v in enumerate((re, re + im, re - im)):
+            A[f1, REFER + 3 * slot + k] = v
+
+
+def product(plan, first, f1, index, slots, A, start):
+    at = f1 + first + index
+    sums = [None] * 3 if start else [A[f1, HELD + 3 * index + k] for k in range(3)]
     for slot in range(slots):
-        sr, si = S[slot, at, 0], S[slot, at, 1]
-        rr, ri = R[slot, f1, 0], R[slot, f1, 1]
-        u = sr * rr + si * ri
-        v = si * rr - sr * ri
-        a, b = (u, v) if a is None else (a + u, b + v)
-    return a, b
-
-
-def add_spectra(plan, first, slots, S, R, held, start):
+        for k in range(3):
+            v = A[at, SIGNAL + 3 * slot + k] * A[f1, REFER + 3 * slot + k]
+            sums[k] = v if sums[k] is None else sums[k] + v
+    return sums
+
+
+def add_spectra(plan, first, slots, A, start):
     step = 4
 
     @pl.loop(0, F1 // step)
     def _(block):
         for k in range(step):
             f1 = block * step + k
-            for owner in range(plan.owners):
-                for i in range(plan.per_owner):
-                    a, b = product(plan, first, f1, owner, i, slots, S, R, held, start)
-                    index = owner * plan.per_owner + i
-                    held[f1, index, 0] = a
-                    held[f1, index, 1] = b
-
-
-def last_spectra(plan, first, slots, S, R, held, high, low):
-    @pl.loop(0, F1)
-    def _(f1):
-        blocks = []
-        for owner in range(plan.owners):
-            found = []
-            for i in range(SUB):
-                if i < plan.per_owner:
-                    found.append(
-                        product(plan, first, f1, owner, i, slots, S, R, held, False)
-                    )
-                else:
-                    found.append((jnp.zeros((SUB, LANES), jnp.float32),) * 2)
-            blocks.append([fold_rows([v[part] for v in found]) for part in range(2)])
-        tall = plan.owners * SUB
-        rows = pl.ds(pl.multiple_of(f1 * tall, tall), tall)
-        for part in range(2):
-            h, l = halves(jnp.concatenate([b[part] for b in blocks], 0))
-            lanes = slice(part * LANES, (part + 1) * LANES)
-            high[rows, lanes] = h
-            low[rows, lanes] = l
+            for index in range(plan.mine):
+                sums = product(plan, first, f1, index, slots, A, start)
+                for which in range(3):
+                    A[f1, HELD + 3 * index + which] = sums[which]
+
+
+def last_spectra(plan, first, slots, A, fold, high, low):
+    step = 2
+    tall = plan.owners * SUB
+
+    @pl.loop(0, F1 // step)
+    def _(block):
+        for k in range(step):
+            f1 = block * step + k
+            for index in range(plan.mine):
+                one, two, three = product(plan, first, f1, index, slots, A, False)
+                row = index // plan.per_owner * SUB + index % plan.per_owner
+                at = row * (SUB + 1)
+                fold[k, 0, at : at + SUB, :] = one - three
+                fold[k, 1, at : at + SUB, :] = one - two
+            rows = pl.ds(pl.multiple_of(f1 * tall, tall), tall)
+            for part in range(2):
+                found = []
+                for owner in range(plan.owners):
+                    at = owner * SUB * (SUB + 1)
+                    parts = [
+                        fold[k, part, pl.ds(at + i, SUB, stride=SUB + 1), :]
+                        for i in range(SUB)
+                    ]
+                    while len(parts) > 1:
+                        parts = [x + y for x, y in zip(parts[::2], parts[1::2])]
+                    found.append(parts[0])
+                h, l = halves(jnp.concatenate(found, 0))
+                lanes = slice(part * LANES, (part + 1) * LANES)
+                high[rows, lanes] = h
+                low[rows, lanes] = l
 
 
 def to_lags(plan, waves, back, high, low, Z, out):
@@ -304,31 +303,13 @@
                 )
 
 
-def schedule(plan):
-    far = plan.far
-    orders, counts = [], []
-    for z in range(far):
-        here, order, count = set(), [], []
-        for k in range(far):
-            here.add(z ^ k)
-            for plane in range(far):
-                for half in range(2):
-                    ready = plane in here and (half or plane == 0 or plane - 1 in here)
-                    if ready and 2 * plane + half not in order:
-                        order.append(2 * plane + half)
-            count.append(len(order))
-        orders.append(order)
-        counts.append(count)
-    return orders, [min(c[k] for c in counts) for k in range(far)]
-
-
-def gather_and_compute(plan, own, every, sems, prepared, compute):
-    send_sems, recv_sems = sems
+def gather_and_compute(plan, own, every, ahead, sems, prepared, transform, add):
+    send_sems, recv_sems, ahead_send, ahead_recv = sems
     cuts, far = plan.cuts, plan.far
     t, c = lax.axis_index("tm"), lax.axis_index("dop")
     z, near = t // 4, t % 4
     beside = [flipped_by(near, k) for k in (1, 2, 3)]
-    levels = [flipped_by(z, k) for k in range(far)]
+    levels = [z] + [k + (k + far - z) // far for k in range(far - 1)]
     fellows = [flipped_by(c, k) for k in range(1, cuts)]
 
     partners = [(z * 4 + n, c) for n in beside]
@@ -339,10 +320,42 @@
         pl.semaphore_signal(
             barrier, inc=1, device_id={"tm": to, "dop": cut}, device_id_type=MESH
         )
-    pl.semaphore_wait(barrier, len(partners))
+    rows = own[0].shape[0]
+    tail = min(rows, ROWS)
+    enders = ROWS // tail
+    ends = (near == 3) & (c >= cuts - enders) & (z < far - 1)
+
+    @pl.when(z > 0)
+    def _():
+        for i in range(enders):
+            pl.semaphore_signal(
+                barrier,
+                inc=1,
+                device_id={"tm": t - near - 1, "dop": cuts - enders + i},
+                device_id_type=MESH,
+            )
+
+    pl.semaphore_wait(barrier, len(partners) + jnp.where(ends, 4 * cuts, 0))
+
+    def forerun(slot, n, cut):
+        which = jnp.maximum(c - (cuts - enders), 0)
+        return pltpu.make_async_remote_copy(
+            src_ref=own[1].at[pl.ds(rows - tail, tail)],
+            dst_ref=ahead.at[pl.ds(pl.multiple_of(which * tail, tail), tail)],
+            send_sem=ahead_send.at[slot],
+            recv_sem=ahead_recv.at[which],
+            device_id={"tm": jnp.minimum(z + 1, far - 1) * 4 + n, "dop": cut},
+            device_id_type=MESH,
+        )
+
+    spots = [(n, cut) for n in range(4) for cut in range(cuts)]
+
+    @pl.when(ends)
+    def _():
+        for slot, (n, cut) in enumerate(spots):
+            forerun(slot, n, cut).start()
 
     sent = []
-    rows = own[0].shape[0]
     pad = (0, ROWS)
 
     def place(which, source):
@@ -383,7 +396,7 @@
                 landed((levels[k] * 4 + n) * cuts + fellow)
 
     me = t * cuts + c
-    for level in levels[:0:-1]:
+    for level in levels[1:]:
         send(me, level * 4 + near, c, True)
     for n in beside:
         send(me, z * 4 + n, c, True)
@@ -403,28 +416,35 @@
             send(source, z * 4 + n, c)
         for fellow in fellows:
             send(source, t, fellow)
-    orders, counts = schedule(plan)
-
-    def group_at(i):
-        group = orders[0][i] + 0 * z
-        for other in range(1, far):
-            group = jnp.where(z == other, orders[other][i], group)
-        return group
-
-    done = 0
+
+    @pl.when(z == 0)
+    def _():
+        ahead[...] = jnp.zeros((ROWS, LANES), jnp.bfloat16)
+
+    @pl.when(z > 0)
+    def _():
+        for i in range(enders):
+            pltpu.make_async_remote_copy(
+                src_ref=own[1].at[pl.ds(rows - tail, tail)],
+                dst_ref=ahead.at[pl.ds(i * tail, tail)],
+                send_sem=ahead_send.at[0],
+                recv_sem=ahead_recv.at[i],
+                device_id={"tm": t, "dop": c},
+                device_id_type=MESH,
+            ).wait_recv()
+
     for k in range(far):
         complete(k)
-        whole = [group_at(i) for i in range(done, counts[k])]
-        if k == far - 1:
-            compute(whole, done == 0, True)
-            break
-        for group in whole[:-1]:
-            compute([group], done == 0, False)
-            done += 1
-        pass_on(k + 1)
-        for group in whole[-1:]:
-            compute([group], done == 0, False)
-            done += 1
+        transform([2 * levels[k], 2 * levels[k] + 1], ahead if k == 0 else None)
+        if k < far - 1:
+            pass_on(k + 1)
+        add(k == 0, k == far - 1)
+
+    @pl.when(ends)
+    def _():
+        for slot, (n, cut) in enumerate(spots):
+            forerun(slot, n, cut).wait_send()
+
     return sent
 
 
@@ -492,13 +512,13 @@
 
 def whole_kernel(plan, s, r, waves_at, forward_at, back_at, out, *scratch):
     (gs, gr, waves, forward, back, tiles) = scratch[:6]
-    drift, even, odd, held = scratch[6:10]
-    stage, high, low, rstage, rhigh, rlow = scratch[10:16]
-    S, R, yhigh, ylow, Z = scratch[16:21]
-    load_sems, gather_sems, deal_sems = scratch[21], scratch[22:24], scratch[24:26]
+    drift, even, odd, A, ahead, fold = scratch[6:12]
+    stage, high, low, rstage, rhigh, rlow = scratch[12:18]
+    yhigh, ylow, Z = scratch[18:21]
+    load_sems, gather_sems, deal_sems = scratch[21], scratch[22:26], scratch[26:28]
     me = lax.axis_index("tm") * plan.cuts + lax.axis_index("dop")
     fine = me // plan.share
-    first = (me % plan.share) * plan.mine
+    first = 0 if plan.share == 1 else (me % plan.share) * plan.mine
     loads = [
         pltpu.make_async_copy(source, target, load_sems.at[i])
         for i, (source, target) in enumerate(
@@ -514,19 +534,23 @@
         for load in loads:
             load.wait()
 
-    def compute(groups, start, last):
+    def transform(groups, before):
         for slot, group in enumerate(groups):
             work = (drift, even, odd, stage, high, low)
-            signal_group(plan, group, slot, gs, waves, forward, work, S)
-            reference_group(
-                plan, group, slot, gr, waves, forward, (rstage, rhigh, rlow), R
-            )
+            signal_group(plan, group, slot, gs, waves, forward, work, A)
+            work = (rstage, rhigh, rlow)
+            head = before if slot == 0 else None
+            reference_group(plan, group, slot, gr, head, waves, forward, work, A)
+
+    def add(start, last):
         if last:
-            last_spectra(plan, first, len(groups), S, R, held, yhigh, ylow)
+            last_spectra(plan, first, 2, A, fold, yhigh, ylow)
         else:
-            add_spectra(plan, first, len(groups), S, R, held, start)
-
-    sent = gather_and_compute(plan, (s, r), (gs, gr), gather_sems, prepared, compute)
+            add_spectra(plan, first, 2, A, start)
+
+    sent = gather_and_compute(
+        plan, (s, r), (gs, gr), ahead, gather_sems, prepared, transform, add
+    )
     to_lags(plan, waves, back, yhigh, ylow, Z, tiles)
     deal(plan, tiles, out, deal_sems)
     for one in sent:
@@ -538,8 +562,9 @@
     tall = plan.owners * SUB
     f32, bf16 = jnp.float32, jnp.bfloat16
     samples = 2 * plan.window // LANES
-    counts = schedule(plan)[1]
-    slots = counts[-1] - counts[-2]
+    slots = 2
+    width = -(-(HELD + 3 * plan.mine) // 4) * 4
+    enders = max(1, ROWS * plan.devices // samples)
     return pl.pallas_call(
         functools.partial(whole_kernel, plan),
         out_shape=jax.ShapeDtypeStruct((plan.fine, 2 * SUB, LANES), bf16),
@@ -556,21 +581,23 @@
             pltpu.VMEM((plan.groups, 2, SUB, LANES), f32),
             pltpu.VMEM((N1, 2, SUB, LANES), f32),
             pltpu.VMEM((N1, 2, SUB, LANES), f32),
-            pltpu.VMEM((F1, plan.mine, 2, SUB, LANES), f32),
-            pltpu.VMEM((SUB * APART + 7, LANES), f32),
-            pltpu.VMEM((F1 * SUB, 2 * LANES), bf16),
-            pltpu.VMEM((F1 * SUB, 2 * LANES), bf16),
-            pltpu.VMEM((SUB * APART + APART + 7, LANES), f32),
-            pltpu.VMEM((F1 * SUB, 2 * LANES), bf16),
-            pltpu.VMEM((F1 * SUB, 2 * LANES), bf16),
-            pltpu.VMEM((slots, F1 + plan.shifts, 2, SUB, LANES), f32),
-            pltpu.VMEM((slots, F1, 2, SUB, LANES), f32),
+            pltpu.VMEM((F1 + plan.shifts, width, SUB, LANES), f32),
+            pltpu.VMEM((ROWS, LANES), bf16),
+            pltpu.VMEM((2, 2, tall * (SUB + 1) + 7, LANES), f32),
+            pltpu.VMEM((slots, SUB * APART + 7, LANES), f32),
+            pltpu.VMEM((slots, F1 * SUB, 2 * LANES), bf16),
+            pltpu.VMEM((slots, F1 * SUB, 2 * LANES), bf16),
+            pltpu.VMEM((slots, SUB * APART + APART + 7, LANES), f32),
+            pltpu.VMEM((slots, F1 * SUB, 2 * LANES), bf16),
+            pltpu.VMEM((slots, F1 * SUB, 2 * LANES), bf16),
             pltpu.VMEM((F1 * tall, 2 * LANES), bf16),
             pltpu.VMEM((F1 * tall, 2 * LANES), bf16),
             pltpu.VMEM((F1 * tall, 2 * LANES), f32),
             pltpu.SemaphoreType.DMA((3,)),
             pltpu.SemaphoreType.DMA((sends_needed(plan),)),
             pltpu.SemaphoreType.DMA((2, plan.devices)),
+            pltpu.SemaphoreType.DMA((4 * plan.cuts,)),
+            pltpu.SemaphoreType.DMA((enders,)),
             pltpu.SemaphoreType.DMA((plan.times, plan.owners)),
             pltpu.SemaphoreType.DMA((plan.fine,)),
         ],

time: 36 us -> 34.4 us (0.956)
  the two profiles are of different devices: /device:TPU:1 before, /device:TPU:0 now
where the time goes in v4:
time: 34.4 us; the launch traced here: 34.1 us
  Pallas kernels  34.1 us (99%)
    pallas_call x1, Pallas kernels, dealt_maps(): pl.pallas_call(functools.partial(whole_kernel, plan), out_shape=jax.Shape...  32 us
    pallas_call x1, Pallas kernels, settled(): pl.pallas_call(functools.partial(settle_kernel, plan), out_shape=jax.Shap...  2.12 us

profile of v4, /device:TPU:0, one launch (start us, length us, event | category | flops | bytes accessed | tf_op | source)
XLA Modules:
  0.0 34.1 jit_solution(12139936255960118714)
XLA Ops:
  0.0 32.0 %shard_map.64.tiles = bf16[32,16,128]{2,1,0:T(8,128)(2,1)} custom-call(bf16[64,128]{1,0:T(8,128)(2,1)} %bitcast.10, bf16[64,128]{1,0:T(8,128)(2,1)} %bitcast.11, bf16[4,256,256]{2,1,0:T(8,128)(2,1)} %constant.8.clone.waves_at, f32[32,2,8,128]{3,2,1,0:T(8,128)} %constant.9.clone.forward_at, f32[32,2,8,128]{3,2,1,0:T(8,128)} %constant.10.clone.back_at), custom_call_target="tpu_custom_call" | custom-call | tf_op jit(solution)/shard_map/pallas_call | solution.py:568
  32.0 2.1 %shard_map.65 = f32[128,2,256]{2,1,0:T(2,128)} custom-call(bf16[32,16,128]{2,1,0:T(8,128)(2,1)} %shard_map.64.tiles, bf16[512,512]{1,0:T(8,128)(2,1)} %constant.11.clone.order), custom_call_target="tpu_custom_call" | custom-call | tf_op jit(solution)/shard_map/pallas_call | solution.py:657

commit v5 on v4

--- a/solution.py
+++ b/solution.py
@@ -177,9 +177,9 @@
     )
 
 
-def signal_group(plan, group, slot, gs, waves, forward, work, A):
+def signal_rows(plan, group, slot, gs, forward, work):
     drift, even, odd, stage, high, low = work
-    stage, high, low = stage.at[slot], high.at[slot], low.at[slot]
+    stage, high, low = stage.at[slot], high.at[slot, 0], low.at[slot, 0]
     start = pl.multiple_of(group * GROUP, GROUP)
     staged(gs[pl.ds(start, GROUP), :], stage)
     here = (drift[group, 0], drift[group, 1])
@@ -187,25 +187,11 @@
     for parity, table in enumerate((even, odd)):
         y = [times_(x[n], (table[n, 0], table[n, 1])) for n in range(N1)]
         turn_and_split(dft16(y, -1), parity, forward, high, low)
-    wide = lanes_turned(high, low, waves, 0)
-    reach = plan.shifts // 2
-    for f1 in range(F1):
-        row = (f1 % 2) * 128 + (f1 // 2) * SUB
-        re = wide[row : row + SUB, :LANES]
-        im = wide[row : row + SUB, LANES:]
-        for k, v in enumerate((re + im, re, im)):
-            A[reach + f1, SIGNAL + 3 * slot + k] = v
-            if f1 < reach:
-                A[reach + f1 + F1, SIGNAL + 3 * slot + k] = pltpu.roll(
-                    v, LANES - 1, 1
-                )
-            if f1 >= F1 - reach:
-                A[reach + f1 - F1, SIGNAL + 3 * slot + k] = pltpu.roll(v, 1, 1)
-
-
-def reference_group(plan, group, slot, gr, before, waves, forward, work, A):
+
+
+def reference_rows(plan, group, slot, gr, before, forward, work):
     stage, high, low = work
-    stage, high, low = stage.at[slot], high.at[slot], low.at[slot]
+    stage, high, low = stage.at[slot], high.at[slot, 1], low.at[slot, 1]
     start = pl.multiple_of(group * GROUP, GROUP)
     if before is None:
         staged(gr[pl.ds(start, GROUP + ROWS), :], stage)
@@ -218,9 +204,26 @@
     turn_and_split(dft16(y, -1), 0, forward, high, low)
     y = [turned(minus(a, b), n, F1, -1) for n, (a, b) in enumerate(zip(now, before))]
     turn_and_split(dft16(y, -1), 1, forward, high, low)
-    wide = lanes_turned(high, low, waves, 0)
+
+
+def group_spectra(plan, slot, waves, high, low, A):
+    tall = F1 * SUB
+    shape = (2 * tall, 2 * LANES)
+    wide = lanes_turned(high[slot].reshape(shape), low[slot].reshape(shape), waves, 0)
+    reach = plan.shifts // 2
     for f1 in range(F1):
         row = (f1 % 2) * 128 + (f1 // 2) * SUB
+        re = wide[row : row + SUB, :LANES]
+        im = wide[row : row + SUB, LANES:]
+        for k, v in enumerate((re + im, re, im)):
+            at = SIGNAL + 3 * slot + k
+            A[reach + f1, at] = v
+            if f1 < reach:
+                A[reach + f1 + F1, at] = pltpu.roll(v, LANES - 1, 1)
+            if f1 >= F1 - reach:
+                A[reach + f1 - F1, at] = pltpu.roll(v, 1, 1)
+    for f1 in range(F1):
+        row = tall + (f1 % 2) * 128 + (f1 // 2) * SUB
         re = wide[row : row + SUB, :LANES]
         im = wide[row : row + SUB, LANES:]
         for k, v in enumerate((re, re + im, re - im)):
@@ -250,67 +253,76 @@
                     A[f1, HELD + 3 * index + which] = sums[which]
 
 
-def last_spectra(plan, first, slots, A, fold, high, low):
+def last_spectra(plan, first, slots, owner, A, fold, high, low):
     step = 2
-    tall = plan.owners * SUB
 
     @pl.loop(0, F1 // step)
     def _(block):
+        kept = []
         for k in range(step):
             f1 = block * step + k
-            for index in range(plan.mine):
+            for i in range(plan.per_owner):
+                index = owner * plan.per_owner + i
                 one, two, three = product(plan, first, f1, index, slots, A, False)
-                row = index // plan.per_owner * SUB + index % plan.per_owner
-                at = row * (SUB + 1)
+                at = i * (SUB + 1)
                 fold[k, 0, at : at + SUB, :] = one - three
                 fold[k, 1, at : at + SUB, :] = one - two
-            rows = pl.ds(pl.multiple_of(f1 * tall, tall), tall)
             for part in range(2):
-                found = []
-                for owner in range(plan.owners):
-                    at = owner * SUB * (SUB + 1)
-                    parts = [
-                        fold[k, part, pl.ds(at + i, SUB, stride=SUB + 1), :]
-                        for i in range(SUB)
-                    ]
-                    while len(parts) > 1:
-                        parts = [x + y for x, y in zip(parts[::2], parts[1::2])]
-                    found.append(parts[0])
-                h, l = halves(jnp.concatenate(found, 0))
-                lanes = slice(part * LANES, (part + 1) * LANES)
-                high[rows, lanes] = h
-                low[rows, lanes] = l
-
-
-def to_lags(plan, waves, back, high, low, Z, out):
-    Z[...] = lanes_turned(high, low, waves, 2)
-    tall = plan.owners * SUB
-    for owner in range(plan.owners):
-        z = []
-        for f1 in range(F1):
-            rows = slice(f1 * tall + owner * SUB, f1 * tall + owner * SUB + SUB)
-            v = (Z[rows, :LANES], Z[rows, LANES:])
-            z.append(times_(v, (back[f1, 0], back[f1, 1])))
-        half = F1 // 2
-        sums = dft16([plus(z[i], z[i + half]) for i in range(half)], 1)
-        gaps = dft16(
-            [turned(minus(z[i], z[i + half]), i, F1, 1) for i in range(half)], 1
-        )
-        for e in range(N1 // 2):
-            for parity, found in enumerate((sums, gaps)):
-                out[2 * e + parity, owner] = jnp.concatenate(found[e], 0).astype(
-                    jnp.bfloat16
-                )
+                found = [
+                    fold[k, part, pl.ds(i, SUB, stride=SUB + 1), :] for i in range(SUB)
+                ]
+                while len(found) > 1:
+                    found = [x + y for x, y in zip(found[::2], found[1::2])]
+                kept.append(found[0])
+        rows = pl.ds(pl.multiple_of(block * step * SUB, step * SUB), step * SUB)
+        for part in range(2):
+            h, l = halves(jnp.concatenate(kept[part::2], 0))
+            lanes = slice(part * LANES, (part + 1) * LANES)
+            high[owner, rows, lanes] = h
+            low[owner, rows, lanes] = l
+
+
+def to_lags(plan, owner, waves, back, high, low, Z, out):
+    Z[owner] = lanes_turned(high[owner], low[owner], waves, 2)
+    z = []
+    for f1 in range(F1):
+        rows = slice(f1 * SUB, f1 * SUB + SUB)
+        v = (Z[owner, rows, :LANES], Z[owner, rows, LANES:])
+        z.append(times_(v, (back[f1, 0], back[f1, 1])))
+    half = F1 // 2
+    sums = dft16([plus(z[i], z[i + half]) for i in range(half)], 1)
+    gaps = dft16([turned(minus(z[i], z[i + half]), i, F1, 1) for i in range(half)], 1)
+    for e in range(N1 // 2):
+        for parity, found in enumerate((sums, gaps)):
+            out[2 * e + parity, owner] = jnp.concatenate(found[e], 0).astype(
+                jnp.bfloat16
+            )
 
 
 def gather_and_compute(plan, own, every, ahead, sems, prepared, transform, add):
-    send_sems, recv_sems, ahead_send, ahead_recv = sems
+    send_sems, recv_sems, ahead_send, ahead_recv, own_sems = sems
     cuts, far = plan.cuts, plan.far
     t, c = lax.axis_index("tm"), lax.axis_index("dop")
     z, near = t // 4, t % 4
     beside = [flipped_by(near, k) for k in (1, 2, 3)]
     levels = [z] + [k + (k + far - z) // far for k in range(far - 1)]
     fellows = [flipped_by(c, k) for k in range(1, cuts)]
+
+    sent = []
+    pad = (0, ROWS)
+    rows = own[0].shape[0]
+    me = t * cuts + c
+
+    def place(which, source):
+        start = pl.multiple_of(source * rows, rows) + pad[which]
+        return every[which].at[pl.ds(pl.multiple_of(start, 16), rows)]
+
+    mine = [
+        pltpu.make_async_copy(own[which], place(which, me), own_sems.at[which])
+        for which in range(2)
+    ]
+    for one in mine:
+        one.start()
 
     partners = [(z * 4 + n, c) for n in beside]
     partners += [(other * 4 + near, c) for other in levels[1:]]
@@ -320,7 +332,6 @@
         pl.semaphore_signal(
             barrier, inc=1, device_id={"tm": to, "dop": cut}, device_id_type=MESH
         )
-    rows = own[0].shape[0]
     tail = min(rows, ROWS)
     enders = ROWS // tail
     ends = (near == 3) & (c >= cuts - enders) & (z < far - 1)
@@ -337,10 +348,12 @@
 
     pl.semaphore_wait(barrier, len(partners) + jnp.where(ends, 4 * cuts, 0))
 
+    last = place(1, me).at[pl.ds(rows - tail, tail)]
+
     def forerun(slot, n, cut):
         which = jnp.maximum(c - (cuts - enders), 0)
         return pltpu.make_async_remote_copy(
-            src_ref=own[1].at[pl.ds(rows - tail, tail)],
+            src_ref=last,
             dst_ref=ahead.at[pl.ds(pl.multiple_of(which * tail, tail), tail)],
             send_sem=ahead_send.at[slot],
             recv_sem=ahead_recv.at[which],
@@ -349,18 +362,13 @@
         )
 
     spots = [(n, cut) for n in range(4) for cut in range(cuts)]
+    for one in mine:
+        one.wait()
 
     @pl.when(ends)
     def _():
         for slot, (n, cut) in enumerate(spots):
             forerun(slot, n, cut).start()
-
-    sent = []
-    pad = (0, ROWS)
-
-    def place(which, source):
-        start = pl.multiple_of(source * rows, rows) + pad[which]
-        return every[which].at[pl.ds(pl.multiple_of(start, 16), rows)]
 
     def copy(which, source, src, to, cut, slot):
         return pltpu.make_async_remote_copy(
@@ -372,16 +380,15 @@
             device_id_type=MESH,
         )
 
-    def send(source, to, cut, mine=False):
+    def send(source, to, cut):
         for which in range(2):
-            src = own[which] if mine else place(which, source)
-            one = copy(which, source, src, to, cut, len(sent))
+            one = copy(which, source, place(which, source), to, cut, len(sent))
             one.start()
             sent.append(one)
 
     def landed(source):
         for which in range(2):
-            copy(which, source, own[which], t, c, 0).wait_recv()
+            copy(which, source, place(which, source), t, c, 0).wait_recv()
 
     def pass_on(k):
         for n in beside:
@@ -395,17 +402,12 @@
             for n in [near] + beside:
                 landed((levels[k] * 4 + n) * cuts + fellow)
 
-    me = t * cuts + c
     for level in levels[1:]:
-        send(me, level * 4 + near, c, True)
+        send(me, level * 4 + near, c)
     for n in beside:
-        send(me, z * 4 + n, c, True)
+        send(me, z * 4 + n, c)
     for fellow in fellows:
-        send(me, t, fellow, True)
-    for which in range(2):
-        every[which][pl.ds(pl.multiple_of(me * rows + pad[which], 16), rows)] = own[
-            which
-        ][...]
+        send(me, t, fellow)
     prepared()
 
     pass_on(0)
@@ -425,7 +427,7 @@
     def _():
         for i in range(enders):
             pltpu.make_async_remote_copy(
-                src_ref=own[1].at[pl.ds(rows - tail, tail)],
+                src_ref=last,
                 dst_ref=ahead.at[pl.ds(i * tail, tail)],
                 send_sem=ahead_send.at[0],
                 recv_sem=ahead_recv.at[i],
@@ -453,7 +455,7 @@
     return 2 * ((far - 1) + far * (3 + 4 * fellows))
 
 
-def deal(plan, tiles, out, sems):
+def dealer(plan, tiles, out, sems):
     send_sems, recv_sems = sems
     times = plan.times
     t, c = lax.axis_index("tm"), lax.axis_index("dop")
@@ -473,10 +475,9 @@
             device_id_type=MESH,
         )
 
-    for step in range(times - 1, 0, -1):
-        for owner in range(plan.owners):
+    def start(owner):
+        for step in range(times - 1, 0, -1):
             copy(step, owner).start()
-    for owner in range(plan.owners):
         itself = base + owner == c
 
         @pl.when(jnp.logical_not(itself))
@@ -487,35 +488,37 @@
         def _():
             out[fine] = tiles[t * plan.lags // LANES, owner]
 
-    for source in range(plan.fine):
-
-        @pl.when((fine != source) | jnp.logical_not(to_me))
-        def _():
-            pltpu.make_async_remote_copy(
-                src_ref=tiles.at[0, 0],
-                dst_ref=out.at[source],
-                send_sem=send_sems.at[0, 0],
-                recv_sem=recv_sems.at[source],
-                device_id={"tm": t, "dop": c},
-                device_id_type=MESH,
-            ).wait_recv()
-
-    for step in range(1, times):
+    def finish():
+        for source in range(plan.fine):
+
+            @pl.when((fine != source) | jnp.logical_not(to_me))
+            def _():
+                pltpu.make_async_remote_copy(
+                    src_ref=tiles.at[0, 0],
+                    dst_ref=out.at[source],
+                    send_sem=send_sems.at[0, 0],
+                    recv_sem=recv_sems.at[source],
+                    device_id={"tm": t, "dop": c},
+                    device_id_type=MESH,
+                ).wait_recv()
+
+        for step in range(1, times):
+            for owner in range(plan.owners):
+                copy(step, owner).wait_send()
         for owner in range(plan.owners):
-            copy(step, owner).wait_send()
-    for owner in range(plan.owners):
-
-        @pl.when(base + owner != c)
-        def _():
-            copy(0, owner).wait_send()
+
+            @pl.when(base + owner != c)
+            def _():
+                copy(0, owner).wait_send()
+
+    return start, finish
 
 
 def whole_kernel(plan, s, r, waves_at, forward_at, back_at, out, *scratch):
     (gs, gr, waves, forward, back, tiles) = scratch[:6]
     drift, even, odd, A, ahead, fold = scratch[6:12]
-    stage, high, low, rstage, rhigh, rlow = scratch[12:18]
-    yhigh, ylow, Z = scratch[18:21]
-    load_sems, gather_sems, deal_sems = scratch[21], scratch[22:26], scratch[26:28]
+    stage, rstage, high, low, yhigh, ylow, Z = scratch[12:19]
+    load_sems, gather_sems, deal_sems = scratch[19], scratch[20:25], scratch[25:27]
     me = lax.axis_index("tm") * plan.cuts + lax.axis_index("dop")
     fine = me // plan.share
     first = 0 if plan.share == 1 else (me % plan.share) * plan.mine
@@ -526,6 +529,9 @@
         )
     ]
 
+    if plan.per_owner < SUB:
+        fold[...] = jnp.zeros(fold.shape, jnp.float32)
+
     def prepared():
         for load in loads:
             load.start()
@@ -537,29 +543,32 @@
     def transform(groups, before):
         for slot, group in enumerate(groups):
             work = (drift, even, odd, stage, high, low)
-            signal_group(plan, group, slot, gs, waves, forward, work, A)
-            work = (rstage, rhigh, rlow)
+            signal_rows(plan, group, slot, gs, forward, work)
+            work = (rstage, high, low)
             head = before if slot == 0 else None
-            reference_group(plan, group, slot, gr, head, waves, forward, work, A)
+            reference_rows(plan, group, slot, gr, head, forward, work)
+            group_spectra(plan, slot, waves, high, low, A)
 
     def add(start, last):
         if last:
-            last_spectra(plan, first, 2, A, fold, yhigh, ylow)
+            deal = dealer(plan, tiles, out, deal_sems)
+            for owner in range(plan.owners):
+                last_spectra(plan, first, 2, owner, A, fold, yhigh, ylow)
+                to_lags(plan, owner, waves, back, yhigh, ylow, Z, tiles)
+                deal[0](owner)
+            deal[1]()
         else:
             add_spectra(plan, first, 2, A, start)
 
     sent = gather_and_compute(
         plan, (s, r), (gs, gr), ahead, gather_sems, prepared, transform, add
     )
-    to_lags(plan, waves, back, yhigh, ylow, Z, tiles)
-    deal(plan, tiles, out, deal_sems)
     for one in sent:
         one.wait_send()
 
 
 def dealt_maps(plan, s, r):
     waves, forward, back = tables(plan)
-    tall = plan.owners * SUB
     f32, bf16 = jnp.float32, jnp.bfloat16
     samples = 2 * plan.window // LANES
     slots = 2
@@ -568,8 +577,7 @@
     return pl.pallas_call(
         functools.partial(whole_kernel, plan),
         out_shape=jax.ShapeDtypeStruct((plan.fine, 2 * SUB, LANES), bf16),
-        in_specs=[pl.BlockSpec(memory_space=pltpu.VMEM)] * 2
-        + [pl.BlockSpec(memory_space=pl.ANY)] * 3,
+        in_specs=[pl.BlockSpec(memory_space=pltpu.MemorySpace.HBM)] * 5,
         out_specs=pl.BlockSpec(memory_space=pltpu.VMEM),
         scratch_shapes=[
             pltpu.VMEM((samples, LANES), bf16),
@@ -583,21 +591,20 @@
             pltpu.VMEM((N1, 2, SUB, LANES), f32),
             pltpu.VMEM((F1 + plan.shifts, width, SUB, LANES), f32),
             pltpu.VMEM((ROWS, LANES), bf16),
-            pltpu.VMEM((2, 2, tall * (SUB + 1) + 7, LANES), f32),
+            pltpu.VMEM((2, 2, SUB * (SUB + 1) + 7, LANES), f32),
             pltpu.VMEM((slots, SUB * APART + 7, LANES), f32),
-            pltpu.VMEM((slots, F1 * SUB, 2 * LANES), bf16),
-            pltpu.VMEM((slots, F1 * SUB, 2 * LANES), bf16),
             pltpu.VMEM((slots, SUB * APART + APART + 7, LANES), f32),
-            pltpu.VMEM((slots, F1 * SUB, 2 * LANES), bf16),
-            pltpu.VMEM((slots, F1 * SUB, 2 * LANES), bf16),
-            pltpu.VMEM((F1 * tall, 2 * LANES), bf16),
-            pltpu.VMEM((F1 * tall, 2 * LANES), bf16),
-            pltpu.VMEM((F1 * tall, 2 * LANES), f32),
+            pltpu.VMEM((slots, 2, F1 * SUB, 2 * LANES), bf16),
+            pltpu.VMEM((slots, 2, F1 * SUB, 2 * LANES), bf16),
+            pltpu.VMEM((plan.owners, F1 * SUB, 2 * LANES), bf16),
+            pltpu.VMEM((plan.owners, F1 * SUB, 2 * LANES), bf16),
+            pltpu.VMEM((plan.owners, F1 * SUB, 2 * LANES), f32),
             pltpu.SemaphoreType.DMA((3,)),
             pltpu.SemaphoreType.DMA((sends_needed(plan),)),
             pltpu.SemaphoreType.DMA((2, plan.devices)),
             pltpu.SemaphoreType.DMA((4 * plan.cuts,)),
             pltpu.SemaphoreType.DMA((enders,)),
+            pltpu.SemaphoreType.DMA((2,)),
             pltpu.SemaphoreType.DMA((plan.times, plan.owners)),
             pltpu.SemaphoreType.DMA((plan.fine,)),
         ],

time: 34.4 us -> 33.2 us (0.965)
  the two profiles are of different devices: /device:TPU:0 before, /device:TPU:1 now
where the time goes in v5:
time: 33.2 us; the launch traced here: 33 us
  Pallas kernels  33 us (99%)
    pallas_call x1, Pallas kernels, dealt_maps(): pl.pallas_call(functools.partial(whole_kernel, plan), out_shape=jax.Shape...  30.9 us
    pallas_call x1, Pallas kernels, settled(): pl.pallas_call(functools.partial(settle_kernel, plan), out_shape=jax.Shap...  2.12 us

profile of v5, /device:TPU:1, one launch (start us, length us, event | category | flops | bytes accessed | tf_op | source)
XLA Modules:
  0.0 33.0 jit_solution(16081146962223896588)
XLA Ops:
  0.0 30.9 %shard_map.64.tiles = bf16[32,16,128]{2,1,0:T(8,128)(2,1)} custom-call(bf16[64,128]{1,0:T(8,128)(2,1)} %bitcast.10, bf16[64,128]{1,0:T(8,128)(2,1)} %bitcast.11, bf16[4,256,256]{2,1,0:T(8,128)(2,1)} %constant.8.clone.waves_at, f32[32,2,8,128]{3,2,1,0:T(8,128)} %constant.9.clone.forward_at, f32[32,2,8,128]{3,2,1,0:T(8,128)} %constant.10.clone.back_at), custom_call_target="tpu_custom_call" | custom-call | tf_op jit(solution)/shard_map/pallas_call | solution.py:577
  30.9 2.1 %shard_map.65 = f32[128,2,256]{2,1,0:T(2,128)} custom-call(bf16[32,16,128]{2,1,0:T(8,128)(2,1)} %shard_map.64.tiles, bf16[512,512]{1,0:T(8,128)(2,1)} %constant.11.clone.order), custom_call_target="tpu_custom_call" | custom-call | tf_op jit(solution)/shard_map/pallas_call | solution.py:664

commit v6 on v5

--- a/solution.py
+++ b/solution.py
@@ -402,19 +402,21 @@
             for n in [near] + beside:
                 landed((levels[k] * 4 + n) * cuts + fellow)
 
-    for level in levels[1:]:
+    for i in range(1, far):
+        level = jnp.where(z < far // 2, levels[far - i], levels[i])
         send(me, level * 4 + near, c)
-    for n in beside:
+    for n in beside[::-1]:
         send(me, z * 4 + n, c)
     for fellow in fellows:
         send(me, t, fellow)
     prepared()
 
-    pass_on(0)
-    for level in levels[1:]:
+    for k, level in enumerate(levels[1:]):
+        if k == 1:
+            pass_on(0)
         source = (level * 4 + near) * cuts + c
         landed(source)
-        for n in beside:
+        for n in beside[::-1]:
             send(source, z * 4 + n, c)
         for fellow in fellows:
             send(source, t, fellow)

time: 33.2 us -> 32.6 us (0.982)
  Pallas kernels: 33 us -> 32.3 us
    pallas_call x1, Pallas kernels: 30.9 us -> 30.2 us  [dealt_maps(): pl.pallas_call(functools.partial(whole_kernel, plan), out_shape=jax.Shape...]
where the time goes in v6:
time: 32.6 us; the launch traced here: 32.4 us
  Pallas kernels  32.3 us (99%)
    pallas_call x1, Pallas kernels, dealt_maps(): pl.pallas_call(functools.partial(whole_kernel, plan), out_shape=jax.Shape...  30.2 us
    pallas_call x1, Pallas kernels, settled(): pl.pallas_call(functools.partial(settle_kernel, plan), out_shape=jax.Shap...  2.12 us

profile of v6, /device:TPU:1, one launch (start us, length us, event | category | flops | bytes accessed | tf_op | source)
XLA Modules:
  0.0 32.4 jit_solution(132360689191362556)
XLA Ops:
  0.0 30.2 %shard_map.64.tiles = bf16[32,16,128]{2,1,0:T(8,128)(2,1)} custom-call(bf16[64,128]{1,0:T(8,128)(2,1)} %bitcast.10, bf16[64,128]{1,0:T(8,128)(2,1)} %bitcast.11, bf16[4,256,256]{2,1,0:T(8,128)(2,1)} %constant.8.clone.waves_at, f32[32,2,8,128]{3,2,1,0:T(8,128)} %constant.9.clone.forward_at, f32[32,2,8,128]{3,2,1,0:T(8,128)} %constant.10.clone.back_at), custom_call_target="tpu_custom_call" | custom-call | tf_op jit(solution)/shard_map/pallas_call | solution.py:579
  30.2 2.1 %shard_map.65 = f32[128,2,256]{2,1,0:T(2,128)} custom-call(bf16[32,16,128]{2,1,0:T(8,128)(2,1)} %shard_map.64.tiles, bf16[512,512]{1,0:T(8,128)(2,1)} %constant.11.clone.order), custom_call_target="tpu_custom_call" | custom-call | tf_op jit(solution)/shard_map/pallas_call | solution.py:666

commit v7 on v6

--- a/solution.py
+++ b/solution.py
@@ -365,11 +365,6 @@
     for one in mine:
         one.wait()
 
-    @pl.when(ends)
-    def _():
-        for slot, (n, cut) in enumerate(spots):
-            forerun(slot, n, cut).start()
-
     def copy(which, source, src, to, cut, slot):
         return pltpu.make_async_remote_copy(
             src_ref=src,
@@ -409,6 +404,11 @@
         send(me, z * 4 + n, c)
     for fellow in fellows:
         send(me, t, fellow)
+    @pl.when(ends)
+    def _():
+        for slot, (n, cut) in enumerate(spots):
+            forerun(slot, n, cut).start()
+
     prepared()
 
     for k, level in enumerate(levels[1:]):

time: 32.6 us -> 32.1 us (0.985)
  Pallas kernels: 32.3 us -> 31.8 us
    pallas_call x1, Pallas kernels: 30.2 us -> 29.7 us  [dealt_maps(): pl.pallas_call(functools.partial(whole_kernel, plan), out_shape=jax.Shape...]
where the time goes in v7:
time: 32.1 us; the launch traced here: 31.8 us
  Pallas kernels  31.8 us (99%)
    pallas_call x1, Pallas kernels, dealt_maps(): pl.pallas_call(functools.partial(whole_kernel, plan), out_shape=jax.Shape...  29.7 us
    pallas_call x1, Pallas kernels, settled(): pl.pallas_call(functools.partial(settle_kernel, plan), out_shape=jax.Shap...  2.12 us

profile of v7, /device:TPU:1, one launch (start us, length us, event | category | flops | bytes accessed | tf_op | source)
XLA Modules:
  0.0 31.8 jit_solution(11117032119574544715)
XLA Ops:
  0.0 29.7 %shard_map.64.tiles = bf16[32,16,128]{2,1,0:T(8,128)(2,1)} custom-call(bf16[64,128]{1,0:T(8,128)(2,1)} %bitcast.10, bf16[64,128]{1,0:T(8,128)(2,1)} %bitcast.11, bf16[4,256,256]{2,1,0:T(8,128)(2,1)} %constant.8.clone.waves_at, f32[32,2,8,128]{3,2,1,0:T(8,128)} %constant.9.clone.forward_at, f32[32,2,8,128]{3,2,1,0:T(8,128)} %constant.10.clone.back_at), custom_call_target="tpu_custom_call" | custom-call | tf_op jit(solution)/shard_map/pallas_call | solution.py:579
  29.7 2.1 %shard_map.65 = f32[128,2,256]{2,1,0:T(2,128)} custom-call(bf16[32,16,128]{2,1,0:T(8,128)(2,1)} %shard_map.64.tiles, bf16[512,512]{1,0:T(8,128)(2,1)} %constant.11.clone.order), custom_call_target="tpu_custom_call" | custom-call | tf_op jit(solution)/shard_map/pallas_call | solution.py:666
